TPU v7x, 32 devices: a whole 2x2x4 slice. The times are simulated.
32 devices in a mesh: groups: 2 (over y), blk: 4 (over z), ulysses: 2 (over x), cfg: 2 (over core).
Axes of the slice: x: 2, y: 2, z: 4, core: 2. Of those that a mesh axis runs over, the one named last changes fastest.
Arguments:
- img_tokens: bfloat16 [2, 2, 512, 2432], P('cfg', 'groups', ('blk', 'ulysses')), parts along dimension 1, may hold values from -72 to 72
- text_tokens: bfloat16 [2, 2, 48, 2432], P('cfg', 'groups', ('blk', 'ulysses')), parts along dimension 1, may hold values from -6 to 6
- text_lengths: int32 [2, 2], P('cfg', 'groups'), parts along dimension 1, may hold values from 12 to 48
- timestep: int32 [2], P('groups'), parts along dimension 0, may hold values from 0 to 999
- pooled: float32 [2, 2, 2432], P(None, 'groups'), parts along dimension 1, may hold values from -6 to 6
- time_weight: bfloat16 [256, 2432], replicated, may hold values from -0.375 to 0.375
- time_second: bfloat16 [2432, 2432], P(None, ('blk', 'ulysses', 'cfg')), may hold values from -0.125 to 0.125
- mod_weight: bfloat16 [2432, 24320], P(None, ('blk', 'ulysses', 'cfg')), may hold values from -0.125 to 0.125
- proj_weight: bfloat16 [5, 2432, 2048], P(None, None, ('ulysses', 'cfg')), may hold values from -0.125 to 0.125
- out_weight: bfloat16 [2048, 2432], P(('ulysses', 'cfg')), may hold values from -0.125 to 0.125
- expand_weight: bfloat16 [2432, 7168], P('blk', ('ulysses', 'cfg')), may hold values from -0.125 to 0.125
- reduce_weight: bfloat16 [7168, 2432], P(('ulysses', 'cfg'), 'blk'), may hold values from -0.0625 to 0.0625
- qk_gain: float32 [3, 64], replicated, may hold values from 0.5 to 10
- final_weight: bfloat16 [2432, 64], replicated, may hold values from -0.125 to 0.125
Outputs:
- guided: float32 [2, 16, 16, 128], P('groups', None, ('blk', 'ulysses', 'cfg')), parts along dimension 0
There are 2 independent parts, one for each index of `groups`. A program takes and returns all parts, laid end to end along the dimension named above; an argument that names none is the same for every part. Nothing has to cross between parts.
All inputs are finite; a program needn't handle non-finite values.
Results may differ from a plain program's by a relative error of at most 0.011.
The roundings to bfloat16 on the way count: a program that leaves them out, or rounds other values in their place, can miss the bound.
Values may be sent and summed in bfloat16 or wider, within the bound.
A program may use at most 192 MiB of HBM per device.

v0:
```python
import math

import jax
import jax.numpy as jnp
from jax import lax
from jax.sharding import PartitionSpec as P

GUIDANCE = 3.5
LN_EPS = 1e-06
RMS_EPS = 1e-06
NEG_FILL = -1e30
block_keys = 512


def from_partner(value, axis, stride):
    mask = 2**stride
    pairs = [(source, source ^ mask) for source in range(lax.axis_size(axis))]
    return lax.ppermute(value, axis, pairs)


def sinusoid(timestep, feature_count):
    half_width = feature_count // 2
    frequency = jnp.exp(-math.log(10000.0) * jnp.arange(half_width, dtype=jnp.float32) / half_width)
    angles = timestep.astype(jnp.float32)[:, None] * frequency[None, :]
    return jnp.concatenate([jnp.cos(angles), jnp.sin(angles)], axis=1)


def layer_norm(values):
    average = jnp.mean(values, axis=-1, keepdims=True)
    centred = values - average
    variance = jnp.mean(centred * centred, axis=-1, keepdims=True)
    return centred * lax.rsqrt(variance + LN_EPS)


def modulate(values, shift, scale):
    return (layer_norm(values.astype(jnp.float32)) * (1.0 + scale) + shift).astype(jnp.bfloat16)


def rms_heads(values, gain):
    head_size = gain.shape[0]
    shaped = values.reshape(values.shape[:-1] + (values.shape[-1] // head_size, head_size))
    inverse = lax.rsqrt(jnp.mean(shaped * shaped, axis=-1, keepdims=True) + RMS_EPS)
    return (shaped * inverse * gain).reshape(values.shape).astype(jnp.bfloat16)


def finish(img_proj, txt_proj, gain_rows):
    img_set = jnp.stack(
        [
            rms_heads(img_proj[0], gain_rows[0]),
            rms_heads(img_proj[1], gain_rows[1]),
            img_proj[2].astype(jnp.bfloat16),
        ]
    )
    txt_set = jnp.stack([rms_heads(txt_proj[0], gain_rows[2]), txt_proj[1].astype(jnp.bfloat16)])
    return (img_set, txt_set)


def attend(state_now, query_heads, key_rows, value_rows, usable, scale):
    running_max, running_total, running_sum = state_now
    prompts, query_count, head_count, head_size = query_heads.shape
    key_count = key_rows.shape[1]
    key_heads = key_rows.reshape(prompts, key_count, head_count, head_size)
    value_heads = value_rows.reshape(prompts, key_count, head_count, head_size)
    scores = (
        jnp.einsum("pqhd,pkhd->phqk", query_heads, key_heads, preferred_element_type=jnp.float32)
        * scale
    )
    allowed = usable[:, None, None, :]
    block_max = jnp.max(jnp.where(allowed, scores, NEG_FILL), axis=3)
    new_max = jnp.maximum(running_max, block_max)
    weights = jnp.where(allowed, jnp.exp(scores - new_max[..., None]), 0.0)
    factor = jnp.exp(running_max - new_max)
    running_total = running_total * factor + jnp.sum(weights, axis=3)
    update = jnp.einsum(
        "phqk,pkhd->pqhd",
        weights.astype(jnp.bfloat16),
        value_heads,
        preferred_element_type=jnp.float32,
    )
    running_sum = running_sum * factor.transpose(0, 2, 1)[..., None] + update
    return (new_max, running_total, running_sum)


def attend_rows(state_now, query_heads, key_value, usable, scale):
    key_count = key_value.shape[2]
    for first_key in range(0, key_count, block_keys):
        last_key = min(first_key + block_keys, key_count)
        state_now = attend(
            state_now,
            query_heads,
            key_value[0, :, first_key:last_key],
            key_value[1, :, first_key:last_key],
            usable[:, first_key:last_key],
            scale,
        )
    return state_now


def make_fold(query_heads, lengths, img_span, txt_span, scale):
    span = img_span + txt_span

    def fold(state_now, kv_piece, first_row):
        key_count = kv_piece.shape[2]
        positions = jnp.arange(key_count, dtype=jnp.int32)
        shard_index = positions // span
        offset = positions - shard_index * span
        text_slot = offset - img_span
        usable = (offset < img_span)[None, :] | (text_slot[None, :] < lengths[:, None])
        return attend_rows(state_now, query_heads, kv_piece, usable, scale)

    return fold


def body(
    img_tokens,
    text_tokens,
    text_lengths,
    timestep,
    pooled,
    time_weight,
    time_second,
    mod_weight,
    proj_weight,
    out_weight,
    expand_weight,
    reduce_weight,
    qk_gain,
    final_weight,
):
    model_width = img_tokens.shape[3]
    prompts = img_tokens.shape[1]
    head_size = qk_gain.shape[1]
    branch = lax.axis_index("cfg")
    sinusoid_rows = sinusoid(timestep, time_weight.shape[0]).astype(jnp.bfloat16)
    time_hidden = jax.nn.silu(
        jnp.dot(sinusoid_rows, time_weight, preferred_element_type=jnp.float32)
    ).astype(jnp.bfloat16)
    time_part = jnp.dot(time_hidden, time_second, preferred_element_type=jnp.float32)
    time_embed = lax.all_gather(time_part, ("blk", "ulysses", "cfg"), axis=1, tiled=True)
    acted = jax.nn.silu(time_embed[None] + pooled).astype(jnp.bfloat16)
    mod_part = jnp.einsum("bpd,dc->bpc", acted, mod_weight, preferred_element_type=jnp.float32)
    mod_all = lax.all_gather(mod_part, ("blk", "ulysses", "cfg"), axis=2, tiled=True)
    own_mod = lax.dynamic_index_in_dim(mod_all, branch, 0, keepdims=False).reshape(
        prompts, 10, model_width
    )
    image_rows = img_tokens[0]
    text_rows = text_tokens[0]
    lengths = text_lengths[0]
    h_img = modulate(image_rows, own_mod[:, 0:1], own_mod[:, 1:2])
    h_txt = modulate(text_rows, own_mod[:, 4:5], own_mod[:, 3:4])
    rows_img, rows_txt = (
        lax.all_gather(h_img, "ulysses", axis=1, tiled=True),
        lax.all_gather(h_txt, "ulysses", axis=1, tiled=True),
    )
    img_span = rows_img.shape[1]
    txt_span = rows_txt.shape[1]
    img_count = 3 * prompts * img_span
    weight_piece = lax.all_gather(proj_weight, "cfg", axis=2, tiled=True)
    columns = weight_piece.shape[2]
    img_part = jnp.einsum(
        "prd,jdc->jprc", rows_img, weight_piece[0:3], preferred_element_type=jnp.float32
    )
    txt_part = jnp.einsum(
        "prd,jdc->jprc", rows_txt, weight_piece[3:5], preferred_element_type=jnp.float32
    )
    stacked_rows = jnp.concatenate(
        [img_part.reshape(-1, columns), txt_part.reshape(-1, columns)], axis=0
    )
    img_proj = stacked_rows[:img_count].reshape(3, prompts, img_span, -1)
    txt_proj = stacked_rows[img_count:].reshape(2, prompts, txt_span, -1)
    img_set, txt_set = finish(img_proj, txt_proj, qk_gain)
    inner_local = img_set.shape[3]
    head_count = inner_local // head_size
    query_heads = img_set[0].reshape(prompts, img_span, head_count, head_size)
    scale = 1.0 / math.sqrt(head_size)
    start_state = (
        jnp.full((prompts, head_count, img_span), NEG_FILL, jnp.float32),
        jnp.zeros((prompts, head_count, img_span), jnp.float32),
        jnp.zeros((prompts, img_span, head_count, head_size), jnp.float32),
    )
    text_kv = lax.all_gather(jnp.stack([txt_set[0], txt_set[1]]), "blk", axis=2, tiled=True)
    slot_usable = jnp.arange(text_kv.shape[2], dtype=jnp.int32)[None, :] < lengths[:, None]
    text_state = attend_rows(start_state, query_heads, text_kv, slot_usable, scale)
    image_kv = jnp.stack([img_set[1], img_set[2]])
    fold = make_fold(query_heads, lengths, img_span, 0, scale)
    final_state = fold(
        text_state, lax.all_gather(image_kv, "blk", axis=2, tiled=True), jnp.int32(0)
    )
    running_max, running_total, running_sum = final_state
    mixed = (running_sum / running_total.transpose(0, 2, 1)[..., None]).astype(jnp.bfloat16)
    mixed_rows = mixed.reshape(prompts, img_span, inner_local).transpose(1, 0, 2)
    out_gathered = lax.all_gather(out_weight, "cfg", axis=0, tiled=True)
    token_count = image_rows.shape[1]
    segment = mixed_rows
    attended = lax.psum_scatter(
        jnp.einsum("rpc,cd->rpd", segment, out_gathered, preferred_element_type=jnp.float32).astype(
            jnp.bfloat16
        ),
        "ulysses",
        scatter_dimension=0,
        tiled=True,
    ).astype(jnp.float32)
    attended = attended.transpose(1, 0, 2)
    residual = image_rows.astype(jnp.float32) + own_mod[:, 2:3] * attended
    feed_input = modulate(residual, own_mod[:, 7:8], own_mod[:, 8:9]).reshape(
        prompts * token_count, model_width
    )
    feed_all = lax.all_gather(feed_input, ("ulysses", "cfg"), axis=0, tiled=True)
    columns = feed_all
    pre_active = jnp.dot(
        columns,
        lax.all_gather(expand_weight, "blk", axis=0, tiled=True),
        preferred_element_type=jnp.float32,
    )
    feed_hidden = jax.nn.gelu(pre_active, approximate=True).astype(jnp.bfloat16)
    reduce_full = lax.all_gather(reduce_weight, "blk", axis=1, tiled=True)
    segment = feed_hidden
    feed_out = lax.psum_scatter(
        jnp.dot(segment, reduce_full, preferred_element_type=jnp.float32).astype(jnp.bfloat16),
        ("ulysses", "cfg"),
        scatter_dimension=0,
        tiled=True,
    ).astype(jnp.float32)
    second_residual = residual + own_mod[:, 9:10] * feed_out.reshape(
        prompts, token_count, model_width
    )
    final_rows = modulate(second_residual, own_mod[:, 6:7], own_mod[:, 5:6])
    noise = jnp.einsum("prd,dc->prc", final_rows, final_weight, preferred_element_type=jnp.float32)
    latent_channels = final_weight.shape[1] // 4
    noise_own = noise.reshape(prompts, token_count, 2, 2, latent_channels).transpose(0, 4, 2, 1, 3)
    noise_own = noise_own.reshape(prompts, latent_channels, 2, 2 * token_count)
    kept_row = lax.dynamic_slice_in_dim(noise_own, branch, 1, 2)
    sent_row = lax.dynamic_slice_in_dim(noise_own, 1 - branch, 1, 2)
    noise_pair = from_partner(sent_row, "cfg", 0)
    noise_cond = jnp.where(branch == 0, kept_row, noise_pair)
    noise_uncond = jnp.where(branch == 0, noise_pair, kept_row)
    return noise_uncond + GUIDANCE * (noise_cond - noise_uncond)


def solution(mesh):
    in_specs = (
        P("cfg", "groups", ("blk", "ulysses"), None),
        P("cfg", "groups", ("blk", "ulysses"), None),
        P("cfg", "groups"),
        P("groups"),
        P(None, "groups", None),
        P(),
        P(None, ("blk", "ulysses", "cfg")),
        P(None, ("blk", "ulysses", "cfg")),
        P(None, None, ("ulysses", "cfg")),
        P(("ulysses", "cfg"), None),
        P("blk", ("ulysses", "cfg")),
        P(("ulysses", "cfg"), "blk"),
        P(),
        P(),
    )
    out_specs = P("groups", None, ("blk", "ulysses", "cfg"), None)
    return jax.shard_map(body, mesh=mesh, in_specs=in_specs, out_specs=out_specs, check_vma=False)
```

profile of v0, /device:TPU:0, one launch (start us, length us, event | category | flops | bytes accessed | tf_op | source)
XLA Modules:
  0.0 583.4 jit_solution(9271355319539368346)
XLA Ops:
  6.6 0.7 all-gather.10.cloned.1.call-update
  8.1 0.3 convolution_reduce_fusion
  8.4 0.6 dynamic-slice.1
  9.7 0.3 fusion.110
  10.0 0.2 dynamic-update-slice
  10.2 62.9 %all-reduce = f32[2432]{0:T(1024)S(1)} all-reduce(f32[2432]{0:T(1024)S(1)} %dynamic-update-slice), channel_id=2, replica_groups=mesh['groups'=2,'blk'=4,'ulysses'=2,'cfg'=2] {'blk','ulysses','cfg'}, use_global_device_ids=true, to_apply=%add | all-reduce | flops 2432 | bytes 19456
  73.2 5.2 convolution_bitcast_fusion
  78.3 17.7 %all-gather.2 = f32[16,1520,2]{1,2,0:T(2,128)S(1)} all-gather(f32[1,1520,2]{1,2,0:T(2,128)S(1)} %convolution_bitcast_fusion), channel_id=3, replica_groups=mesh['groups'=2,'blk'=4,'ulysses'=2,'cfg'=2] {'blk','ulysses','cfg'}, dimensions={0}, use_global_device_ids=true | all-gather | bytes 206720 | tf_op jit(solution)/shard_map/all_gather | solution.py:142
  96.0 0.3 reshape.1011
  96.3 0.3 dynamic-slice_reduce_fusion
  96.7 0.1 convert_reduce_fusion
  96.9 0.3 fusion.50
  97.1 0.3 slice_reduce_fusion.4
  97.4 0.2 fusion.53
  97.6 10.5 %all_gather.35 = bf16[1,128,2432]{2,1,0:T(8,128)(2,1)S(1)} all-gather(bf16[1,64,2432]{2,1,0:T(8,128)(2,1)S(1)} %fusion.53), channel_id=1, replica_groups=mesh['groups'=2,'blk'=4,'ulysses'=2,'cfg'=2] {'ulysses'}, dimensions={1}, use_global_device_ids=true | all-gather | bytes 933888 | tf_op jit(solution)/shard_map/all_gather | solution.py:152
  108.2 6.5 %fusion.21 = f32[3,1,128,1024]{3,2,0,1:T(8,128)S(1)} fusion(bf16[5,2432,1024]{2,1,0:T(8,128)(2,1)} %all-gather.10.cloned.1.call-done, bf16[1,128,2432]{2,1,0:T(8,128)(2,1)S(1)} %all_gather.35), kind=kOutput, calls=%fused_computation.26 | convolution fusion | flops 1912602624 | bytes 17137664 | tf_op jit(solution)/shard_map/prd,jdc->jprc/dot_general | solution.py:160
  114.7 0.2 copy.67
  115.0 1.0 copy.68
  116.0 2.0 slice_multiply_fusion.2
  118.0 0.9 pad_maximum_fusion
  118.9 0.7 all-gather.14.cloned.1.call-update
  119.7 0.2 fusion.77
  119.8 0.2 multiply_reduce_fusion.2
  120.1 0.1 add_convert_fusion.2
  120.9 4.9 all_gather.37
  125.8 5.3 fusion.32
  131.3 0.1 reduce_sum.126
  131.5 0.1 mul.478
  131.7 15.8 %all_gather.38 = bf16[2,1,48,1024]{3,0,1,2:T(2,128)(2,1)S(1)} all-gather(bf16[2,1,12,1024]{3,0,1,2:T(2,128)(2,1)S(1)} %copy.64), channel_id=1, replica_groups=mesh['groups'=2,'blk'=4,'ulysses'=2,'cfg'=2] {'blk'}, dimensions={2}, use_global_device_ids=true | all-gather | bytes 245760 | tf_op jit(solution)/shard_map/all_gather | solution.py:181
  147.4 0.8 slice_reduce_fusion
  148.3 0.2 reshape.995
  148.4 0.2 copy.61
  148.7 0.2 copy.60
  148.9 0.2 reshape.996
  149.1 0.3 select_reduce_fusion.1
  149.4 16.9 %all-gather.12.cloned.1.call-done = bf16[2,1,512,1024]{3,2,0,1:T(8,128)(2,1)} async-done(((bf16[2,1,128,1024]{3,2,0,1:T(8,128)(2,1)}), bf16[2,1,512,1024]{3,2,0,1:T(8,128)(2,1)}) %all-gather.12.cloned.1.call-update) | async-done | bytes 2097168 | tf_op jit(solution)/shard_map/all_gather | solution.py:187
  166.4 3.1 fusion.107
  169.4 1.5 copy.69
  170.9 2.3 copy.70
  173.2 0.9 select_reduce_fusion
  174.2 0.1 fusion.59
  174.3 1.1 fusion.5
  175.4 0.3 fusion.31
  175.7 1.1 fusion.38
  176.7 4.8 all-gather.14.cloned.1.call-done
  181.6 4.1 fusion.4
  185.8 0.5 all-gather.18.cloned.1.call-update
  186.4 0.5 all-gather.20.cloned.1.call-update
  186.9 15.8 %reduce-scatter.3.cloned.1.call-done = bf16[64,1,2432]{2,0,1:T(8,128)(2,1)} async-done(((bf16[128,1,2432]{2,0,1:T(8,128)(2,1)}), bf16[64,1,2432]{2,0,1:T(8,128)(2,1)}) %reduce-scatter.3.cloned.1.call-update) | async-done | bytes 311312 | tf_op jit(solution)/shard_map/reduce_scatter | solution.py:195
  202.8 1.2 fusion.58
  204.0 1.2 multiply_reduce_fusion.1
  205.2 1.9 add_convert_fusion.1
  207.1 0.3 reduce-scatter.5.cloned.1.call-start
  207.4 151.8 %all-gather.18.cloned.1.call-done = bf16[2432,1792]{1,0:T(8,128)(2,1)} async-done(((bf16[608,1792]{1,0:T(8,128)(2,1)}), bf16[2432,1792]{1,0:T(8,128)(2,1)}) %all-gather.18.cloned.1.call-update) | async-done | bytes 8716304 | tf_op jit(solution)/shard_map/all_gather | solution.py:212
  359.2 154.6 %all-gather.20.cloned.1.call-done = bf16[1792,2432]{0,1:T(8,128)(2,1)} async-done(((bf16[1792,608]{0,1:T(8,128)(2,1)}), bf16[1792,2432]{0,1:T(8,128)(2,1)}) %all-gather.20.cloned.1.call-update) | async-done | bytes 8716304 | tf_op jit(solution)/shard_map/all_gather | solution.py:216
  513.8 17.6 %all-gather.16.cloned.1.call-done = bf16[256,2432]{1,0:T(8,128)(2,1)} async-done(((bf16[64,2432]{1,0:T(8,128)(2,1)}), bf16[256,2432]{1,0:T(8,128)(2,1)}) %all-gather.16.cloned.1.call-update) | async-done | bytes 1245200 | tf_op jit(solution)/shard_map/all_gather | solution.py:208
  531.4 13.0 %convolution_convert_fusion = bf16[256,2432]{1,0:T(8,128)(2,1)} fusion(bf16[1792,2432]{0,1:T(8,128)(2,1)} %all-gather.20.cloned.1.call-done, bf16[256,2432]{1,0:T(8,128)(2,1)} %all-gather.16.cloned.1.call-done, bf16[2432,1792]{1,0:T(8,128)(2,1)} %all-gather.18.cloned.1.call-done), kind=kOutput, calls=%fused_computation.6 | convolution fusion | flops 4467490816 | bytes 19922944 | tf_op jit(solution)/shard_map/dot_general | solution.py:219
  544.4 26.2 %reduce-scatter.5.cloned.1.call-done = bf16[64,2432]{1,0:T(8,128)(2,1)} async-done(((bf16[256,2432]{1,0:T(8,128)(2,1)}), bf16[64,2432]{1,0:T(8,128)(2,1)}) %reduce-scatter.5.cloned.1.call-update) | async-done | bytes 311312 | tf_op jit(solution)/shard_map/reduce_scatter | solution.py:218
  570.6 1.2 fusion.105
  571.8 1.3 multiply_reduce_fusion
  573.1 1.4 convolution_bitcast_fusion.2
  574.5 0.1 copy.71
  574.8 1.1 collective-permute-done
  575.9 0.6 multiply_add_fusion.1
  (81 shorter events, 1.5 us)
Async XLA Ops:
  6.5 1.5 copy-start
  6.5 1.9 copy-start.11
  6.5 3.1 copy-start.6
  6.5 66.5 %copy-start.8 = (f32[2,1,2432]{2,1,0:T(1,128)S(1)}, f32[2,1,2432]{2,1,0:T(1,128)}, u32[]{:S(2)}) copy-start(f32[2,1,2432]{2,1,0:T(1,128)} %param.18) | copy-start | bytes 58372
  6.5 101.6 %all-gather.10.cloned.1.call-start = ((), (), s32[]{:S(2)}) async-start(), calls=%async_computation.2 | async-start | bytes 37355520 | tf_op jit(solution)/shard_map/all_gather | solution.py:158
  7.3 159.1 %all-gather.12.cloned.1.call-start = ((), (), s32[]{:S(2)}) async-start(), calls=%async_computation.3 | async-start | bytes 2621440 | tf_op jit(solution)/shard_map/all_gather | solution.py:187
  73.1 23.5 %copy-start.9 = (f32[3,64]{1,0:T(4,128)S(1)}, f32[3,64]{1,0:T(4,128)}, u32[]{:S(2)}) copy-start(f32[3,64]{1,0:T(4,128)} %param.26) | copy-start | bytes 2308
  73.1 23.6 %copy-start.2 = (bf16[1,1,64,2432]{3,2,1,0:T(8,128)(2,1)S(1)}, bf16[1,1,64,2432]{3,2,1,0:T(8,128)(2,1)}, u32[]{:S(2)}) copy-start(bf16[1,1,64,2432]{3,2,1,0:T(8,128)(2,1)} %param.14) | copy-start | bytes 933892
  115.0 4.7 copy-start.7
  118.9 62.7 %all-gather.14.cloned.1.call-start = ((), (), s32[]{:S(2)}) async-start(), calls=%async_computation.4 | async-start | bytes 7471104 | tf_op jit(solution)/shard_map/all_gather | solution.py:192
  119.6 83.2 %reduce-scatter.3.cloned.1.call-start = ((), (), s32[]{:S(2)}) async-start(), calls=%async_computation.5 | async-start | bytes 933888 | tf_op jit(solution)/shard_map/reduce_scatter | solution.py:195
  125.8 22.6 %copy-start.4 = (f32[1,1,128,1024]{3,2,0,1:T(8,128)S(1)}, f32[1,1,128,1024]{3,2,0,1:T(8,128)}, u32[]{:S(2)}) copy-start(f32[1,1,128,1024]{3,2,0,1:T(8,128)} %get-tuple-element.21) | copy-start | bytes 1572868
  174.1 1.5 copy-start.5
  185.7 173.5 %all-gather.18.cloned.1.call-start = ((), (), s32[]{:S(2)}) async-start(), calls=%async_computation.7 | async-start | bytes 10895360 | tf_op jit(solution)/shard_map/all_gather | solution.py:212
  186.3 327.5 %all-gather.20.cloned.1.call-start = ((), (), s32[]{:S(2)}) async-start(), calls=%async_computation.8 | async-start | bytes 10895360 | tf_op jit(solution)/shard_map/all_gather | solution.py:216
  186.9 344.5 %all-gather.16.cloned.1.call-start = ((), (), s32[]{:S(2)}) async-start(), calls=%async_computation.6 | async-start | bytes 1556480 | tf_op jit(solution)/shard_map/all_gather | solution.py:208
  207.1 363.5 %copy-start.3 = (bf16[64,1,2432]{2,0,1:T(8,128)(2,1)S(1)}, bf16[64,1,2432]{2,0,1:T(8,128)(2,1)}, u32[]{:S(2)}) copy-start(bf16[64,1,2432]{2,0,1:T(8,128)(2,1)} %reduce-scatter.3.cloned.1.call-done) | copy-start | bytes 933892
  207.1 366.0 %copy-start.10 = (bf16[2432,64]{0,1:T(8,128)(2,1)S(1)}, bf16[2432,64]{0,1:T(8,128)(2,1)}, u32[]{:S(2)}) copy-start(bf16[2432,64]{0,1:T(8,128)(2,1)} %param.27) | copy-start | bytes 933892
  207.1 363.4 %reduce-scatter.5.cloned.1.call-start = ((), (), s32[]{:S(2)}) async-start(), calls=%async_computation.9 | async-start | bytes 1556480 | tf_op jit(solution)/shard_map/reduce_scatter | solution.py:218
  531.4 45.1 %copy-start.1 = (bf16[256,2432]{1,0:T(8,128)(2,1)S(1)}, bf16[256,2432]{1,0:T(8,128)(2,1)}, u32[]{:S(2)}) copy-start(bf16[256,2432]{1,0:T(8,128)(2,1)} %param.19) | copy-start | bytes 3735556
  574.7 1.2 collective-permute-start
Sparse Core Ops, SparseCore 0:
  8.9 42.6 all-gather.9
  119.0 47.3 all-gather.11
  167.9 13.6 all-gather.13
  185.8 16.8 reduce-scatter.2
  204.2 154.9 all-gather.17
  360.6 153.1 all-gather.19
  515.4 15.9 all-gather.15
  544.5 26.0 reduce-scatter.4
where the time goes:
time: 584 us; the launch traced here: 583 us
  waiting for transfers between devices  391 us (67%)
  blocking collectives  112 us (19%)
  matrix products  38.7 us (7%)
  between operations  16 us (3%)
  other arithmetic  13.3 us (2%)
  local copies, waits for them, and re-layouts  11.8 us (2%)
    all_gather x1, waiting for transfers between devices, body(): reduce_full = lax.all_gather(reduce_weight, 'blk', axis=1, tiled=True)  155 us
    all_gather x1, waiting for transfers between devices, body(): lax.all_gather(expand_weight, 'blk', axis=0, tiled=True)  152 us
    unnamed x1, blocking collectives  62.9 us
    reduce_scatter x1, waiting for transfers between devices, body(): lax.psum_scatter(jnp.dot(segment, reduce_full, preferred_element_type=jnp...  26.2 us
    all_gather x1, blocking collectives, body(): lax.all_gather(mod_part, ('blk', 'ulysses', 'cfg'), axis=2, tiled=True)  17.7 us
    all_gather x1, waiting for transfers between devices, body(): lax.all_gather(feed_input, ('ulysses', 'cfg'), axis=0, tiled=True)  17.6 us
    all_gather x1, waiting for transfers between devices, body(): lax.all_gather(image_kv, 'blk', axis=2, tiled=True)  16.9 us
    reduce_scatter x1, waiting for transfers between devices, body(): lax.psum_scatter(jnp.einsum('rpc,cd->rpd', segment, out_gathered, preferr...  15.8 us
  transfers between devices with their start and end apart: 9, of which 8 were waited for; matrix products, arithmetic and copies ran while one was open for 5% of the time, Pallas kernels for 0%

commit v1 on v0

v1 whole, which is shorter than its diff:
```python
import functools
import math

import jax
import jax.numpy as jnp
from jax import lax
from jax.experimental import pallas as pl
from jax.experimental.pallas import tpu as pltpu
from jax.sharding import PartitionSpec as P

GUIDANCE = 3.5
LN_EPS = 1e-06
RMS_EPS = 1e-06
NEG_FILL = -1e30
MESH = pl.DeviceIdType.MESH


def from_partner(value, axis, stride):
    mask = 2**stride
    pairs = [(source, source ^ mask) for source in range(lax.axis_size(axis))]
    return lax.ppermute(value, axis, pairs)


def sinusoid(timestep, feature_count):
    half_width = feature_count // 2
    frequency = jnp.exp(-math.log(10000.0) * jnp.arange(half_width, dtype=jnp.float32) / half_width)
    angles = timestep.astype(jnp.float32)[:, None] * frequency[None, :]
    return jnp.concatenate([jnp.cos(angles), jnp.sin(angles)], axis=1)


def layer_norm(values):
    average = jnp.mean(values, axis=-1, keepdims=True)
    centred = values - average
    variance = jnp.mean(centred * centred, axis=-1, keepdims=True)
    return centred * lax.rsqrt(variance + LN_EPS)


def modulate(values, shift, scale):
    return (layer_norm(values.astype(jnp.float32)) * (1.0 + scale) + shift).astype(jnp.bfloat16)


def rms_heads(values, gain):
    head_size = gain.shape[0]
    shaped = values.reshape(values.shape[:-1] + (values.shape[-1] // head_size, head_size))
    inverse = lax.rsqrt(jnp.mean(shaped * shaped, axis=-1, keepdims=True) + RMS_EPS)
    return (shaped * inverse * gain).reshape(values.shape).astype(jnp.bfloat16)


def flat_position(axes):
    position = 0
    for axis in axes:
        position = position * lax.axis_size(axis) + lax.axis_index(axis)
    return position


def coordinates(position, axes):
    found = {}
    for axis in reversed(axes):
        size = lax.axis_size(axis)
        found[axis] = lax.rem(position, size)
        position = position // size
    return found


def count_of(axes):
    return math.prod(lax.axis_size(axis) for axis in axes)


def direct_kernel(axes, swap, x_ref, o_ref, send_sem, recv_sem, local_sem):
    count = count_of(axes)
    me = flat_position(axes)
    barrier = pltpu.get_barrier_semaphore()

    def greet(step, carry):
        peer = lax.rem(me + step, count)
        pl.semaphore_signal(
            barrier, inc=1, device_id=coordinates(peer, axes), device_id_type=MESH
        )
        return carry

    lax.fori_loop(1, count, greet, 0)
    own = pltpu.make_async_copy(x_ref.at[me] if swap else x_ref, o_ref.at[me], local_sem)
    own.start()
    pl.semaphore_wait(barrier, count - 1)

    def outgoing(step):
        peer = lax.rem(me + step, count)
        return pltpu.make_async_remote_copy(
            src_ref=x_ref.at[peer] if swap else x_ref,
            dst_ref=o_ref.at[me],
            send_sem=send_sem.at[step],
            recv_sem=recv_sem.at[step],
            device_id=coordinates(peer, axes),
            device_id_type=MESH,
        )

    def incoming(step):
        source = lax.rem(me - step + count, count)
        return pltpu.make_async_remote_copy(
            src_ref=x_ref.at[source] if swap else x_ref,
            dst_ref=o_ref.at[source],
            send_sem=send_sem.at[step],
            recv_sem=recv_sem.at[step],
            device_id=coordinates(source, axes),
            device_id_type=MESH,
        )

    def begin(step, carry):
        outgoing(step).start()
        return carry

    def finish(step, carry):
        incoming(step).wait_recv()
        outgoing(step).wait_send()
        return carry

    lax.fori_loop(1, count, begin, 0)
    lax.fori_loop(1, count, finish, 0)
    own.wait()


def direct(value, axes, swap, collective_id, name):
    count = count_of(axes)
    shape = value.shape if swap else (count,) + value.shape
    return pl.pallas_call(
        functools.partial(direct_kernel, axes, swap),
        out_shape=jax.ShapeDtypeStruct(shape, value.dtype),
        in_specs=[pl.BlockSpec(memory_space=pltpu.VMEM)],
        out_specs=pl.BlockSpec(memory_space=pltpu.VMEM),
        scratch_shapes=[
            pltpu.SemaphoreType.DMA((count,)),
            pltpu.SemaphoreType.DMA((count,)),
            pltpu.SemaphoreType.DMA,
        ],
        compiler_params=pltpu.CompilerParams(collective_id=collective_id, has_side_effects=True),
        cost_estimate=pl.CostEstimate(
            flops=0, bytes_accessed=4 * math.prod(shape) + 4000000, transcendentals=0
        ),
        name=name,
    )(value)


def quad_kernel(
    chunks, x_ref, o_ref, send_u, recv_u, send_c, recv_c, send_f, recv_f, local_sem
):
    size = lax.axis_size("ulysses")
    row = lax.axis_index("ulysses")
    core = lax.axis_index("cfg")
    me = row * 2 + core
    partner = {"ulysses": row, "cfg": 1 - core}
    barrier = pltpu.get_barrier_semaphore()
    for step in range(1, size):
        pl.semaphore_signal(
            barrier,
            inc=1,
            device_id={"ulysses": lax.rem(row + step, size), "cfg": core},
            device_id_type=MESH,
        )
    pl.semaphore_signal(barrier, inc=1, device_id=partner, device_id_type=MESH)
    own = pltpu.make_async_copy(x_ref, o_ref.at[me], local_sem)
    own.start()
    pl.semaphore_wait(barrier, size)

    def across(step, chunk):
        return pltpu.make_async_remote_copy(
            src_ref=x_ref.at[chunk],
            dst_ref=o_ref.at[me, chunk],
            send_sem=send_u.at[step, chunk],
            recv_sem=recv_u.at[step, chunk],
            device_id={"ulysses": lax.rem(row + step, size), "cfg": core},
            device_id_type=MESH,
        )

    def landed(step, chunk):
        source = lax.rem(row - step + size, size)
        return pltpu.make_async_remote_copy(
            src_ref=x_ref.at[chunk],
            dst_ref=o_ref.at[source * 2 + core, chunk],
            send_sem=send_u.at[step, chunk],
            recv_sem=recv_u.at[step, chunk],
            device_id={"ulysses": source, "cfg": core},
            device_id_type=MESH,
        )

    def forward(step, chunk, side):
        source = lax.rem(row - step + size, size)
        return pltpu.make_async_remote_copy(
            src_ref=o_ref.at[source * 2 + side, chunk],
            dst_ref=o_ref.at[source * 2 + side, chunk],
            send_sem=send_f.at[step, chunk],
            recv_sem=recv_f.at[step, chunk],
            device_id=partner,
            device_id_type=MESH,
        )

    def beside(slot):
        return pltpu.make_async_remote_copy(
            src_ref=x_ref,
            dst_ref=o_ref.at[slot],
            send_sem=send_c,
            recv_sem=recv_c,
            device_id=partner,
            device_id_type=MESH,
        )

    pairs = [(step, chunk) for chunk in range(chunks) for step in range(1, size)]
    for step, chunk in pairs:
        across(step, chunk).start()
    beside(me).start()
    for step, chunk in pairs:
        landed(step, chunk).wait_recv()
        forward(step, chunk, core).start()
    for step, chunk in pairs:
        across(step, chunk).wait_send()
        forward(step, chunk, core).wait_send()
        forward(step, chunk, 1 - core).wait_recv()
    beside(me).wait_send()
    beside(row * 2 + 1 - core).wait_recv()
    own.wait()


def quad_gather(value, collective_id, name):
    size = lax.axis_size("ulysses")
    chunks = value.shape[0]
    shape = (size * 2,) + value.shape
    grid_sem = pltpu.SemaphoreType.DMA((size, chunks))
    return pl.pallas_call(
        functools.partial(quad_kernel, chunks),
        out_shape=jax.ShapeDtypeStruct(shape, value.dtype),
        in_specs=[pl.BlockSpec(memory_space=pl.ANY)],
        out_specs=pl.BlockSpec(memory_space=pl.ANY),
        scratch_shapes=[
            grid_sem,
            grid_sem,
            pltpu.SemaphoreType.DMA,
            pltpu.SemaphoreType.DMA,
            grid_sem,
            grid_sem,
            pltpu.SemaphoreType.DMA,
        ],
        compiler_params=pltpu.CompilerParams(collective_id=collective_id, has_side_effects=True),
        cost_estimate=pl.CostEstimate(
            flops=0, bytes_accessed=8 * math.prod(shape) + 4000000, transcendentals=0
        ),
        name=name,
    )(value)


def ring_rows(piece, axis):
    size = lax.axis_size(axis)
    me = lax.axis_index(axis)
    rows = piece.shape[0]
    up = [(source, (source + 1) % size) for source in range(size)]
    down = [(source, (source - 1) % size) for source in range(size)]
    whole = jnp.zeros((size * rows,) + piece.shape[1:], piece.dtype)

    def place(whole, part, owner, offset):
        return lax.dynamic_update_slice_in_dim(whole, part, owner * rows + offset, 0)

    whole = place(whole, piece, me, 0)
    upward = downward = piece
    for step in range(1, (size - 1) // 2 + 1):
        upward = lax.ppermute(upward, axis, up)
        downward = lax.ppermute(downward, axis, down)
        whole = place(whole, upward, lax.rem(me - step + size, size), 0)
        whole = place(whole, downward, lax.rem(me + step, size), 0)
    if size % 2 == 0:
        half = rows // 2 if size > 2 else rows
        far = lax.rem(me + size // 2, size)
        whole = place(whole, lax.ppermute(upward[:half], axis, up), far, 0)
        if half < rows:
            whole = place(whole, lax.ppermute(downward[half:], axis, down), far, half)
    return whole


def body(
    img_tokens,
    text_tokens,
    text_lengths,
    timestep,
    pooled,
    time_weight,
    time_second,
    mod_weight,
    proj_weight,
    out_weight,
    expand_weight,
    reduce_weight,
    qk_gain,
    final_weight,
):
    model_width = img_tokens.shape[3]
    prompts = img_tokens.shape[1]
    head_size = qk_gain.shape[1]
    branches = pooled.shape[0]
    branch = lax.axis_index("cfg")
    everyone = ("blk", "ulysses", "cfg")
    near = ("ulysses", "cfg")
    blocks = lax.axis_size("blk")
    sides = lax.axis_size("ulysses")
    expand_full = ring_rows(expand_weight, "blk")
    sinusoid_rows = sinusoid(timestep, time_weight.shape[0]).astype(jnp.bfloat16)
    time_hidden = jax.nn.silu(
        jnp.dot(sinusoid_rows, time_weight, preferred_element_type=jnp.float32)
    ).astype(jnp.bfloat16)
    time_part = jnp.dot(time_hidden, time_second, preferred_element_type=jnp.float32)
    time_width = time_part.shape[1]
    first = direct(
        jnp.concatenate([time_part, text_lengths[0][:, None].astype(jnp.float32)], axis=1),
        everyone,
        False,
        0,
        "gather_time",
    )
    time_embed = first[:, :, :time_width].transpose(1, 0, 2).reshape(prompts, -1)
    lengths = first[:branches, :, time_width].astype(jnp.int32)
    acted = jax.nn.silu(time_embed[None] + pooled).astype(jnp.bfloat16)
    mod_part = jnp.einsum("bpd,dc->bpc", acted, mod_weight, preferred_element_type=jnp.float32)
    mod_all = direct(mod_part, everyone, False, 1, "gather_mod")
    own_mod = lax.dynamic_index_in_dim(mod_all, branch, 1, keepdims=False)
    own_mod = own_mod.transpose(1, 0, 2).reshape(prompts, 10, model_width)
    image_rows = img_tokens[0]
    text_rows = text_tokens[0]
    token_count = image_rows.shape[1]
    slot_count = text_rows.shape[1]
    h_img = modulate(image_rows, own_mod[:, 0:1], own_mod[:, 1:2])
    h_txt = modulate(text_rows, own_mod[:, 4:5], own_mod[:, 3:4])
    rows_all = quad_gather(
        jnp.concatenate([h_img, h_txt], axis=1), 2, "gather_rows"
    )
    rows_all = rows_all.reshape(sides, branches, prompts, token_count + slot_count, model_width)
    rows_img = rows_all[:, :, :, :token_count]
    rows_txt = rows_all[:, :, :, token_count:]
    img_proj = jnp.einsum(
        "ubprd,jdc->jubprc", rows_img, proj_weight[0:3], preferred_element_type=jnp.float32
    )
    txt_proj = jnp.einsum(
        "ubprd,jdc->jubprc", rows_txt, proj_weight[3:5], preferred_element_type=jnp.float32
    )
    queries = rms_heads(img_proj[0], qk_gain[0])
    img_kv = jnp.stack([rms_heads(img_proj[1], qk_gain[1]), img_proj[2].astype(jnp.bfloat16)])
    txt_kv = jnp.stack([rms_heads(txt_proj[0], qk_gain[2]), txt_proj[1].astype(jnp.bfloat16)])
    inner_local = queries.shape[-1]
    head_count = inner_local // head_size
    own_kv = jnp.concatenate([img_kv, txt_kv], axis=4)
    all_kv = lax.all_gather(own_kv, "blk", axis=0, tiled=False)
    span = token_count + slot_count
    all_kv = all_kv.reshape(
        blocks, 2, sides, branches, prompts, span, head_count, head_size
    )
    query_heads = queries.reshape(sides, branches, prompts, token_count, head_count, head_size)
    scale = 1.0 / math.sqrt(head_size)
    scores = (
        jnp.einsum(
            "ubpqhd,zvbpkhd->bphuqzvk",
            query_heads,
            all_kv[:, 0],
            preferred_element_type=jnp.float32,
        )
        * scale
    )
    place = jnp.arange(span, dtype=jnp.int32) - token_count
    slot = (
        jnp.arange(blocks * sides, dtype=jnp.int32).reshape(blocks, sides, 1) * slot_count + place
    )
    allowed = (place < 0) | (slot < lengths[:, :, None, None, None])
    allowed = allowed[:, :, None, None, None]
    scores = jnp.where(allowed, scores, NEG_FILL)
    largest = jnp.max(scores, axis=(5, 6, 7), keepdims=True)
    weights = jnp.where(allowed, jnp.exp(scores - largest), 0.0)
    denominator = jnp.sum(weights, axis=(5, 6, 7))
    mixed = jnp.einsum(
        "bphuqzvk,zvbpkhd->bphuqd",
        weights.astype(jnp.bfloat16),
        all_kv[:, 1],
        preferred_element_type=jnp.float32,
    )
    mixed = (mixed / denominator[..., None]).astype(jnp.bfloat16)
    mixed_rows = mixed.transpose(3, 0, 1, 4, 2, 5).reshape(-1, inner_local)
    out_terms = jnp.dot(mixed_rows, out_weight, preferred_element_type=jnp.float32)
    out_terms = out_terms.astype(jnp.bfloat16).reshape(
        sides * branches, prompts * token_count, model_width
    )
    out_terms = direct(out_terms, near, True, 3, "swap_out")
    attended = jnp.sum(out_terms.astype(jnp.float32), axis=0)
    attended = attended.reshape(prompts, token_count, model_width)
    residual = image_rows.astype(jnp.float32) + own_mod[:, 2:3] * attended
    feed_input = modulate(residual, own_mod[:, 7:8], own_mod[:, 8:9]).reshape(
        prompts * token_count, model_width
    )
    feed_blocks = lax.all_gather(feed_input, "blk", axis=0, tiled=False)
    feed_all = quad_gather(feed_blocks, 4, "gather_feed").reshape(-1, model_width)
    pre_active = jnp.dot(feed_all, expand_full, preferred_element_type=jnp.float32)
    feed_hidden = jax.nn.gelu(pre_active, approximate=True).astype(jnp.bfloat16)
    feed_terms = jnp.dot(feed_hidden, reduce_weight, preferred_element_type=jnp.float32)
    feed_terms = feed_terms.astype(jnp.bfloat16).reshape(
        sides * branches * blocks, prompts * token_count, -1
    )
    feed_terms = direct(feed_terms, ("ulysses", "cfg", "blk"), True, 5, "swap_feed")
    feed_terms = feed_terms.reshape(sides * branches, blocks, prompts * token_count, -1)
    feed_out = jnp.sum(feed_terms.astype(jnp.float32), axis=0).transpose(1, 0, 2)
    second_residual = residual + own_mod[:, 9:10] * feed_out.reshape(
        prompts, token_count, model_width
    )
    final_rows = modulate(second_residual, own_mod[:, 6:7], own_mod[:, 5:6])
    noise = jnp.einsum("prd,dc->prc", final_rows, final_weight, preferred_element_type=jnp.float32)
    latent_channels = final_weight.shape[1] // 4
    noise_own = noise.reshape(prompts, token_count, 2, 2, latent_channels).transpose(0, 4, 2, 1, 3)
    noise_own = noise_own.reshape(prompts, latent_channels, 2, 2 * token_count)
    kept_row = lax.dynamic_slice_in_dim(noise_own, branch, 1, 2)
    sent_row = lax.dynamic_slice_in_dim(noise_own, 1 - branch, 1, 2)
    noise_pair = from_partner(sent_row, "cfg", 0)
    noise_cond = jnp.where(branch == 0, kept_row, noise_pair)
    noise_uncond = jnp.where(branch == 0, noise_pair, kept_row)
    return noise_uncond + GUIDANCE * (noise_cond - noise_uncond)


def solution(mesh):
    in_specs = (
        P("cfg", "groups", ("blk", "ulysses"), None),
        P("cfg", "groups", ("blk", "ulysses"), None),
        P("cfg", "groups"),
        P("groups"),
        P(None, "groups", None),
        P(),
        P(None, ("blk", "ulysses", "cfg")),
        P(None, ("blk", "ulysses", "cfg")),
        P(None, None, ("ulysses", "cfg")),
        P(("ulysses", "cfg"), None),
        P("blk", ("ulysses", "cfg")),
        P(("ulysses", "cfg"), "blk"),
        P(),
        P(),
    )
    out_specs = P("groups", None, ("blk", "ulysses", "cfg"), None)
    return jax.shard_map(body, mesh=mesh, in_specs=in_specs, out_specs=out_specs, check_vma=False)
```

time: 584 us -> 437 us (0.75)
  waiting for transfers between devices: 391 us -> 154 us
  Pallas kernels: 0 us -> 123 us
  blocking collectives: 112 us -> 0 us
  local copies, waits for them, and re-layouts: 11.8 us -> 66.1 us
  other arithmetic: 13.3 us -> 23.3 us
  starting transfers between devices: 0.57 us -> 8.06 us
  matrix products: 38.7 us -> 45.9 us
    all_gather x6 -> x2, waiting for transfers between devices: 346 us -> 99 us  [the longest x1 99 us: body(): all_kv = lax.all_gather(own_kv, 'blk', axis=0, tiled=False)]
    pallas_call x0 -> x6, Pallas kernels: none -> 123 us  [the longest x4 70.6 us: direct(): pl.pallas_call(functools.partial(direct_kernel, axes, swap), out_shape=ja...]
    unnamed x1 -> x0, blocking collectives: 62.9 us -> none
    ppermute x0 -> x4, waiting for transfers between devices: none -> 53.8 us  [the longest x1 31.9 us: ring_rows(): whole = place(whole, lax.ppermute(upward[:half], axis, up), far, 0)]
    all_gather x4 -> x0, blocking collectives: 48.8 us -> none  [the longest x1 17.7 us: body(): lax.all_gather(mod_part, ('blk', 'ulysses', 'cfg'), axis=2, tiled=True)]
    reduce_scatter x2 -> x0, waiting for transfers between devices: 42 us -> none  [the longest x1 26.2 us: body(): lax.psum_scatter(jnp.dot(segment, reduce_full, preferred_element_type=jnp...]
    reshape x1 -> x4, local copies, waits for them, and re-layouts: 0.02 us -> 12.4 us  [the longest x1 6.87 us: body(): all_kv.reshape(blocks, 2, sides, branches, prompts, span, head_count, hea...]
    dynamic_update_slice x0 -> x5, local copies, waits for them, and re-layouts: none -> 9.87 us  [place(): lax.dynamic_update_slice_in_dim(whole, part, owner * rows + offset, 0)]
  transfers between devices with their start and end apart: 9 -> 7, of which waited for: 8 -> 4; matrix products, arithmetic and copies ran while one was open for 5% -> 15% of each run, Pallas kernels for 0% -> 4%
where the time goes in v1:
time: 437 us; the launch traced here: 436 us
  waiting for transfers between devices  154 us (35%)
  Pallas kernels  123 us (28%)
  local copies, waits for them, and re-layouts  66.1 us (15%)
  matrix products  45.9 us (11%)
  other arithmetic  23.3 us (5%)
  between operations  15.4 us (4%)
  starting transfers between devices  8.06 us (2%)
    all_gather x1, waiting for transfers between devices, body(): all_kv = lax.all_gather(own_kv, 'blk', axis=0, tiled=False)  99 us
    pallas_call x4, Pallas kernels, direct(): pl.pallas_call(functools.partial(direct_kernel, axes, swap), out_shape=ja...  70.6 us
    pallas_call x2, Pallas kernels, quad_gather(): pl.pallas_call(functools.partial(quad_kernel, chunks), out_shape=jax.Shap...  52.3 us
    ppermute x1, waiting for transfers between devices, ring_rows(): whole = place(whole, lax.ppermute(upward[:half], axis, up), far, 0)  31.9 us
    ppermute x1, waiting for transfers between devices, ring_rows(): whole = place(whole, lax.ppermute(downward[half:], axis, down), far, half)  21.8 us
    dot_general x1, matrix products, body(): jnp.dot(feed_hidden, reduce_weight, preferred_element_type=jnp.float32)  18.6 us
    unnamed x36, local copies, waits for them, and re-layouts  10.1 us
    dynamic_update_slice x5, local copies, waits for them, and re-layouts, place(): lax.dynamic_update_slice_in_dim(whole, part, owner * rows + offset, 0)  9.87 us
  transfers between devices with their start and end apart: 7, of which 4 were waited for; matrix products, arithmetic and copies ran while one was open for 15% of the time, Pallas kernels for 4%

profile of v1, /device:TPU:0, one launch (start us, length us, event | category | flops | bytes accessed | tf_op | source)
XLA Modules:
  0.0 435.6 jit_solution(13020006865289216504)
XLA Ops:
  7.4 1.6 convolution_reduce_fusion
  9.7 1.4 fusion.102
  11.1 0.7 pad_maximum_fusion.1.x_ref
  11.8 9.8 %gather_time.1 = f32[16,1,153]{2,1,0:T(1,128)} custom-call(f32[1,153]{1,0:T(1,128)} %pad_maximum_fusion.1.x_ref), custom_call_target="tpu_custom_call" | custom-call | bytes 4009792 | tf_op jit(solution)/shard_map/gather_time/pallas_call | solution.py:125
  21.6 0.8 slice_reduce_fusion
  22.5 0.8 fusion.85
  23.3 5.1 %fusion.90 = f32[2,1520]{1,0:T(2,128)S(1)} fusion(bf16[2432,1520]{0,1:T(8,128)(2,1)} %param.21, bf16[2,1,2432]{2,1,0:T(2,128)(2,1)S(1)} %fusion.85), kind=kOutput, calls=%fused_computation.118 | convolution fusion | flops 14786560 | bytes 7415168 | tf_op jit(solution)/shard_map/bpd,dc->bpc/dot_general | solution.py:318
  29.0 9.6 %gather_mod.1 = f32[16,2,1,1520]{3,2,1,0:T(1,128)} custom-call(f32[2,1,1520]{2,1,0:T(1,128)} %dot_general.55.x_ref), custom_call_target="tpu_custom_call" | custom-call | bytes 4194560 | tf_op jit(solution)/shard_map/gather_mod/pallas_call | solution.py:125
  38.6 1.2 dynamic-slice_reduce_fusion
  39.9 0.9 slice_reduce_fusion.3
  41.9 0.8 pad_maximum_fusion.x_ref
  42.7 13.1 %gather_rows.1 = bf16[4,1,70,2432]{3,2,1,0:T(8,128)(2,1)} custom-call(bf16[1,70,2432]{2,1,0:T(8,128)(2,1)} %pad_maximum_fusion.x_ref), custom_call_target="tpu_custom_call" | custom-call | bytes 9447680 | tf_op jit(solution)/shard_map/gather_rows/pallas_call | solution.py:227
  55.8 5.7 %fusion.27 = f32[3,2,2,1,64,512]{5,4,0,2,1,3:T(8,128)S(1)} fusion(bf16[5,2432,512]{2,1,0:T(8,128)(2,1)} %param.22, bf16[2,2,1,70,2432]{4,3,1,0,2:T(8,128)(2,1)} %bitcast.204), kind=kOutput, calls=%fused_computation.30 | convolution fusion | flops 1912602624 | bytes 10289152 | tf_op jit(solution)/shard_map/ubprd,jdc->jubprc/dot_general | solution.py:334
  61.5 3.9 fusion.35
  65.5 0.7 slice.181
  66.3 1.2 mul.523
  67.5 1.6 reduce_sum.135
  69.2 1.3 mul.524
  70.5 2.3 mul.525
  74.7 2.4 slice_multiply_fusion.2
  77.1 1.8 maximum_maximum_fusion
  79.0 1.7 collective-permute-start
  80.7 2.2 collective-permute-start.1
  82.9 2.2 mul.516
  85.1 1.6 reduce_sum.134
  86.8 1.2 reshape_squeeze.2
  88.0 0.9 convert_reduce_fusion.4
  89.0 99.0 %all-gather.6.cloned.1.call-done = bf16[8,2,2,1,70,512]{5,4,0,2,1,3:T(8,128)(2,1)} async-done(((bf16[2,2,2,1,70,512]{5,4,0,2,1,3:T(8,128)(2,1)}), bf16[8,2,2,1,70,512]{5,4,0,2,1,3:T(8,128)(2,1)}) %all-gather.6.cloned.1.call-update) | async-done | bytes 2293776 | tf_op jit(solution)/shard_map/all_gather | solution.py:346
  188.0 3.9 copy.54
  191.9 6.9 %reshape.1249 = bf16[4,2,2,2,1,70,8,64]{7,6,1,0,5,3,2,4:T(8,128)(2,1)} reshape(bf16[8,2,2,1,70,512]{5,0,4,2,1,3:T(8,128)(2,1)} %copy.54) | data formatting | bytes 4587520 | tf_op jit(solution)/shard_map/reshape | solution.py:348
  198.8 5.3 %fusion.99 = (bf16[4,1,2,2,1,70,8,64]{7,6,1,0,5,3,2,4:T(8,128)(2,1)}, bf16[4,1,2,2,1,70,8,64]{7,6,1,0,5,3,2,4:T(8,128)(2,1)}) fusion(bf16[4,2,2,2,1,70,8,64]{7,6,1,0,5,3,2,4:T(8,128)(2,1)} %reshape.1249), kind=kLoop, calls=%fused_computation.156 | loop fusion | bytes 4587520 | tf_op jit(solution)/shard_map/slice | solution.py:357
  204.1 4.8 %copy.76 = bf16[4,1,2,2,1,70,8,64]{5,7,2,0,6,3,4,1:T(8,128)(2,1)} copy(bf16[4,1,2,2,1,70,8,64]{7,6,1,0,5,3,2,4:T(8,128)(2,1)} %get-tuple-element.19) | data formatting | bytes 2293760
  208.9 5.0 %copy.77 = bf16[4,1,2,2,1,70,8,64]{5,7,0,2,6,3,4,1:T(8,128)(2,1)} copy(bf16[4,1,2,2,1,70,8,64]{7,6,1,0,5,3,2,4:T(8,128)(2,1)} %get-tuple-element.20) | data formatting | bytes 2293760
  214.0 3.8 fusion.3
  217.8 2.8 fusion.12
  220.6 1.2 fusion.44
  222.2 1.0 reshape.1252
  223.2 2.8 convolution_convert_fusion
  226.1 17.7 %swap_out.1 = bf16[4,64,2432]{2,1,0:T(8,128)(2,1)} custom-call(bf16[4,64,2432]{2,1,0:T(8,128)(2,1)} %bitcast.202), custom_call_target="tpu_custom_call" | custom-call | bytes 6490368 | tf_op jit(solution)/shard_map/swap_out/pallas_call | solution.py:125
  243.7 1.5 convert_reduce_fusion.1
  245.7 0.9 add_convert_fusion
  246.7 2.3 slice.131
  249.0 1.3 slice.132
  250.3 4.1 collective-permute-start.3
  254.4 3.9 broadcast_in_dim.23
  258.3 1.5 constant_dynamic-update-slice_fusion.4
  259.8 3.1 constant_dynamic-update-slice_fusion.3
  263.0 3.1 constant_dynamic-update-slice_fusion.2
  266.1 31.9 %collective-permute-done.2 = bf16[304,1792]{1,0:T(8,128)(2,1)S(1)} collective-permute-done((bf16[304,1792]{1,0:T(8,128)(2,1)}, bf16[304,1792]{1,0:T(8,128)(2,1)S(1)}, u32[]{:S(2)}, u32[]{:S(2)}) %collective-permute-start.2) | collective-permute-done | bytes 1089568 | tf_op jit(solution)/shard_map/ppermute | solution.py:270
  298.0 1.1 constant_dynamic-update-slice_fusion.1
  299.0 21.8 %collective-permute-done.3 = bf16[304,1792]{1,0:T(8,128)(2,1)S(1)} collective-permute-done((bf16[304,1792]{1,0:T(8,128)(2,1)S(1)}, bf16[304,1792]{1,0:T(8,128)(2,1)S(1)}, u32[]{:S(2)}, u32[]{:S(2)}) %collective-permute-start.3) | collective-permute-done | bytes 1089568 | tf_op jit(solution)/shard_map/ppermute | solution.py:272
  320.9 1.1 constant_dynamic-update-slice_fusion
  322.0 39.1 %gather_feed.1 = bf16[4,4,64,2432]{3,2,1,0:T(8,128)(2,1)} custom-call(bf16[4,64,2432]{2,1,0:T(8,128)(2,1)} %all-gather.4.cloned.1.call-done.x_ref), custom_call_target="tpu_custom_call" | custom-call | bytes 23922944 | tf_op jit(solution)/shard_map/gather_feed/pallas_call | solution.py:227
  361.1 18.6 %fusion.24 = bf16[1024,608]{0,1:T(8,128)(2,1)S(1)} fusion(bf16[1792,608]{0,1:T(8,128)(2,1)} %param.25, bf16[1024,2432]{1,0:T(8,128)(2,1)} %bitcast.201, bf16[2432,1792]{1,0:T(8,128)(2,1)} %constant_dynamic-update-slice_fusion), kind=kOutput, calls=%fused_computation.29 | convolution fusion | flops 11173986304 | bytes 17121280 | tf_op jit(solution)/shard_map/dot_general | solution.py:395
  379.7 1.7 copy.59
  381.4 33.5 %swap_feed.1 = bf16[16,64,608]{2,1,0:T(8,128)(2,1)} custom-call(bf16[16,64,608]{2,1,0:T(8,128)(2,1)} %bitcast.199), custom_call_target="tpu_custom_call" | custom-call | bytes 6490368 | tf_op jit(solution)/shard_map/swap_feed/pallas_call | solution.py:125
  415.0 1.6 convert_reduce_fusion
  416.6 1.3 copy.60
  417.9 2.3 reshape.1257
  420.1 2.3 reshape.1256
  422.4 1.2 fusion.75
  423.7 1.3 multiply_reduce_fusion
  425.0 1.7 convolution_bitcast_fusion
  427.0 1.1 collective-permute-done.4
  (97 shorter events, 6.2 us)
Async XLA Ops:
  6.5 216.7 %copy-start = (bf16[512,2432]{1,0:T(8,128)(2,1)S(1)}, bf16[512,2432]{1,0:T(8,128)(2,1)}, u32[]{:S(2)}) copy-start(bf16[512,2432]{1,0:T(8,128)(2,1)} %param.23) | copy-start | bytes 7471108
  6.5 181.5 %all-gather.6.cloned.1.call-start = ((), (), s32[]{:S(2)}) async-start(), calls=%async_computation.1 | async-start | bytes 2949120 | tf_op jit(solution)/shard_map/all_gather | solution.py:346
  22.4 18.4 %copy-start.2 = (bf16[1,1,64,2432]{3,2,1,0:T(8,128)(2,1)S(1)}, bf16[1,1,64,2432]{3,2,1,0:T(8,128)(2,1)}, u32[]{:S(2)}) copy-start(bf16[1,1,64,2432]{3,2,1,0:T(8,128)(2,1)} %param.14) | copy-start | bytes 933892
  23.3 18.0 %copy-start.7 = (bf16[1,1,6,2432]{3,2,1,0:T(8,128)(2,1)S(1)}, bf16[1,1,6,2432]{3,2,1,0:T(8,128)(2,1)}, u32[]{:S(2)}) copy-start(bf16[1,1,6,2432]{3,2,1,0:T(8,128)(2,1)} %param.15) | copy-start | bytes 87556
  61.5 4.0 copy-start.5
  67.4 5.4 %copy-start.15 = (f32[3,64]{1,0:T(4,128)S(1)}, f32[3,64]{1,0:T(4,128)}, u32[]{:S(2)}) copy-start(f32[3,64]{1,0:T(4,128)} %param.26) | copy-start | bytes 2308
  78.9 243.0 %all-gather.4.cloned.1.call-start = ((), (), s32[]{:S(2)}) async-start(), calls=%async_computation | async-start | bytes 1556480 | tf_op jit(solution)/shard_map/all_gather | solution.py:391
  79.0 167.7 %collective-permute-start = (bf16[608,1792]{1,0:T(8,128)(2,1)}, bf16[608,1792]{1,0:T(8,128)(2,1)}, u32[]{:S(2)}, u32[]{:S(2)}) collective-permute-start(bf16[608,1792]{1,0:T(8,128)(2,1)} %param.24), channel_id=1, source_target_pairs={{0,4},{4,8},{8,12},{12,0},{1,5},{5,9},{9,13},{13,1},{2,6},{6,10},{... | collective-permute-start | bytes 6537224 | tf_op jit(solution)/shard_map/ppermute | solution.py:263
  80.7 168.4 %collective-permute-start.1 = (bf16[608,1792]{1,0:T(8,128)(2,1)}, bf16[608,1792]{1,0:T(8,128)(2,1)}, u32[]{:S(2)}, u32[]{:S(2)}) collective-permute-start(bf16[608,1792]{1,0:T(8,128)(2,1)} %param.24), channel_id=1, source_target_pairs={{0,12},{4,0},{8,4},{12,8},{1,13},{5,1},{9,5},{13,9},{2,14},{6,2},{... | collective-permute-start | bytes 6537224 | tf_op jit(solution)/shard_map/ppermute | solution.py:264
  204.1 9.9 %copy-start.14 = (f32[64]{0:T(128)S(1)}, f32[64]{0:T(128)}, u32[]{:S(2)}) copy-start(f32[64]{0:T(128)} %get-tuple-element.26) | copy-start | bytes 772
  217.8 2.8 copy-start.6
  223.2 22.1 %copy-start.9 = (f32[2432]{0:T(1024)S(1)}, f32[2432]{0:T(1024)}, u32[]{:S(2)}) copy-start(f32[2432]{0:T(1024)} %get-tuple-element.14) | copy-start | bytes 29188
  226.1 19.7 %copy-start.12 = (f32[2432]{0:T(1024)S(1)}, f32[2432]{0:T(1024)}, u32[]{:S(2)}) copy-start(f32[2432]{0:T(1024)} %get-tuple-element.8) | copy-start | bytes 29188
  226.1 19.7 %copy-start.13 = (f32[2432]{0:T(1024)S(1)}, f32[2432]{0:T(1024)}, u32[]{:S(2)}) copy-start(f32[2432]{0:T(1024)} %get-tuple-element.9) | copy-start | bytes 29188
  245.3 13.1 %copy-start.3 = (f32[64,2432]{1,0:T(8,128)}, f32[64,2432]{1,0:T(8,128)S(1)}, u32[]{:S(2)}) copy-start(f32[64,2432]{1,0:T(8,128)S(1)} %convert_reduce_fusion.1) | copy-start | bytes 1867780
  249.0 49.0 %collective-permute-start.2 = (bf16[304,1792]{1,0:T(8,128)(2,1)}, bf16[304,1792]{1,0:T(8,128)(2,1)S(1)}, u32[]{:S(2)}, u32[]{:S(2)}) collective-permute-start(bf16[304,1792]{1,0:T(8,128)(2,1)} %slice.131), channel_id=1, source_target_pairs={{0,4},{4,8},{8,12},{12,0},{1,5},{5,9},{9,13},{13,1},{2,6},{6,10},{... | collective-permute-start | bytes 3268616 | tf_op jit(solution)/shard_map/ppermute | solution.py:270
  250.3 8.0 %copy-start.4 = (bf16[608,1792]{1,0:T(8,128)(2,1)S(1)}, bf16[608,1792]{1,0:T(8,128)(2,1)}, u32[]{:S(2)}) copy-start(bf16[608,1792]{1,0:T(8,128)(2,1)} %param.24) | copy-start | bytes 6537220
  250.3 70.5 %collective-permute-start.3 = (bf16[304,1792]{1,0:T(8,128)(2,1)S(1)}, bf16[304,1792]{1,0:T(8,128)(2,1)S(1)}, u32[]{:S(2)}, u32[]{:S(2)}) collective-permute-start(bf16[304,1792]{1,0:T(8,128)(2,1)S(1)} %slice.132), channel_id=1, source_target_pairs={{0,12},{4,0},{8,4},{12,8},{1,13},{5,1},{9,5},{13,9},{2,14},{6,2},{... | collective-permute-start | bytes 3268616 | tf_op jit(solution)/shard_map/ppermute | solution.py:272
  381.4 41.0 %copy-start.8 = (f32[2432]{0:T(1024)S(1)}, f32[2432]{0:T(1024)}, u32[]{:S(2)}) copy-start(f32[2432]{0:T(1024)} %get-tuple-element.5) | copy-start | bytes 29188
  415.0 10.0 %copy-start.10 = (f32[2432]{0:T(1024)S(1)}, f32[2432]{0:T(1024)}, u32[]{:S(2)}) copy-start(f32[2432]{0:T(1024)} %get-tuple-element.6) | copy-start | bytes 29188
  415.0 10.0 %copy-start.11 = (f32[2432]{0:T(1024)S(1)}, f32[2432]{0:T(1024)}, u32[]{:S(2)}) copy-start(f32[2432]{0:T(1024)} %get-tuple-element.7) | copy-start | bytes 29188
  416.6 12.1 %copy-start.1 = (bf16[512,2432]{1,0:T(8,128)(2,1)S(1)}, bf16[512,2432]{1,0:T(8,128)(2,1)}, u32[]{:S(2)}) copy-start(bf16[512,2432]{1,0:T(8,128)(2,1)} %param.23) | copy-start | bytes 7471108
  426.9 1.2 collective-permute-start.4
Sparse Core Ops, SparseCore 0:
  79.1 108.9 all-gather.5
  246.8 61.5 all-gather.3

commit v2 on v1

--- a/solution.py
+++ b/solution.py
@@ -7,6 +7,7 @@
 from jax.experimental import pallas as pl
 from jax.experimental.pallas import tpu as pltpu
 from jax.sharding import PartitionSpec as P
+
 
 GUIDANCE = 3.5
 LN_EPS = 1e-06
@@ -119,7 +120,7 @@
     own.wait()
 
 
-def direct(value, axes, swap, collective_id, name):
+def direct(value, axes, swap, collective_id):
     count = count_of(axes)
     shape = value.shape if swap else (count,) + value.shape
     return pl.pallas_call(
@@ -136,7 +137,6 @@
         cost_estimate=pl.CostEstimate(
             flops=0, bytes_accessed=4 * math.prod(shape) + 4000000, transcendentals=0
         ),
-        name=name,
     )(value)
 
 
@@ -219,7 +219,7 @@
     own.wait()
 
 
-def quad_gather(value, collective_id, name):
+def quad_gather(value, collective_id):
     size = lax.axis_size("ulysses")
     chunks = value.shape[0]
     shape = (size * 2,) + value.shape
@@ -242,7 +242,184 @@
         cost_estimate=pl.CostEstimate(
             flops=0, bytes_accessed=8 * math.prod(shape) + 4000000, transcendentals=0
         ),
-        name=name,
+    )(value)
+
+
+def ring_kernel(axis, spread, x_ref, o_ref, hop_s, hop_r, x_s, x_r, c_s, c_r, f_s, f_r, local_sem):
+    size = lax.axis_size(axis)
+    me = lax.axis_index(axis)
+    last = size // 2
+    halved = size % 2 == 0
+    sides = lax.axis_size("ulysses") if spread else 1
+    row = lax.axis_index("ulysses")
+    core = lax.axis_index("cfg")
+    partner = {"ulysses": row, "cfg": 1 - core}
+    base = o_ref.at[row * 2 + core] if spread else o_ref
+
+    def at(offset):
+        return lax.rem(me + offset + size, size)
+
+    def aside(step):
+        return {"ulysses": lax.rem(row + step, sides), "cfg": core}
+
+    barrier = pltpu.get_barrier_semaphore()
+    for way in (1, -1):
+        pl.semaphore_signal(barrier, inc=1, device_id={axis: at(way)}, device_id_type=MESH)
+    if spread:
+        for step in range(1, sides):
+            pl.semaphore_signal(barrier, inc=1, device_id=aside(step), device_id_type=MESH)
+        pl.semaphore_signal(barrier, inc=1, device_id=partner, device_id_type=MESH)
+    own = pltpu.make_async_copy(x_ref, base.at[me], local_sem)
+    own.start()
+    pl.semaphore_wait(barrier, 2 + (sides if spread else 0))
+
+    def part(ref, way, step):
+        if halved and step == last:
+            return ref.at[0 if way == 1 else 1]
+        return ref
+
+    def hop(way, step):
+        slot = at(-way * (step - 1))
+        source = x_ref if step == 1 else base.at[slot]
+        return pltpu.make_async_remote_copy(
+            src_ref=part(source, way, step),
+            dst_ref=part(base.at[slot], way, step),
+            send_sem=hop_s.at[(way + 1) // 2, step],
+            recv_sem=hop_r.at[(way + 1) // 2, step],
+            device_id={axis: at(way)},
+            device_id_type=MESH,
+        )
+
+    def hop_in(way, step):
+        slot = base.at[at(-way * step)]
+        return pltpu.make_async_remote_copy(
+            src_ref=part(slot, way, step),
+            dst_ref=part(slot, way, step),
+            send_sem=hop_s.at[(way + 1) // 2, step],
+            recv_sem=hop_r.at[(way + 1) // 2, step],
+            device_id={axis: at(-way)},
+            device_id_type=MESH,
+        )
+
+    def send(order, offset, step):
+        slot = at(offset)
+        return pltpu.make_async_remote_copy(
+            src_ref=x_ref if order == 0 else base.at[slot],
+            dst_ref=base.at[slot],
+            send_sem=x_s.at[order, step] if step else c_s.at[order],
+            recv_sem=x_r.at[order, step] if step else c_r.at[order],
+            device_id=aside(step) if step else partner,
+            device_id_type=MESH,
+        )
+
+    def across_in(order, offset, step):
+        source = lax.rem(row - step + sides, sides)
+        block = o_ref.at[source * 2 + core, at(offset)]
+        return pltpu.make_async_remote_copy(
+            src_ref=block,
+            dst_ref=block,
+            send_sem=x_s.at[order, step],
+            recv_sem=x_r.at[order, step],
+            device_id=aside(step),
+            device_id_type=MESH,
+        )
+
+    def forward(order, offset, step, side):
+        source = lax.rem(row - step + sides, sides)
+        block = o_ref.at[source * 2 + side, at(offset)]
+        return pltpu.make_async_remote_copy(
+            src_ref=block,
+            dst_ref=block,
+            send_sem=f_s.at[order, step],
+            recv_sem=f_r.at[order, step],
+            device_id=partner,
+            device_id_type=MESH,
+        )
+
+    def beside_in(order, offset):
+        block = o_ref.at[row * 2 + 1 - core, at(offset)]
+        return pltpu.make_async_remote_copy(
+            src_ref=block,
+            dst_ref=block,
+            send_sem=c_s.at[order],
+            recv_sem=c_r.at[order],
+            device_id=partner,
+            device_id_type=MESH,
+        )
+
+    steps = last
+    offsets = [0]
+    for way in (1, -1):
+        hop(way, 1).start()
+    sent = []
+
+    def pass_on(order, offset):
+        if spread:
+            for step in list(range(1, sides)) + [0]:
+                send(order, offset, step).start()
+            sent.append((order, offset))
+
+    def relay(order, offset):
+        for step in range(1, sides):
+            across_in(order, offset, step).wait_recv()
+            forward(order, offset, step, core).start()
+
+    pass_on(0, 0)
+    relayed = 0
+    for step in range(1, steps + 1):
+        final = halved and step == last
+        for way in (1, -1):
+            hop_in(way, step).wait_recv()
+            if step < steps:
+                hop(way, step + 1).start()
+            if not final:
+                offsets.append(-way * step)
+                pass_on(len(offsets) - 1, offsets[-1])
+        if final:
+            offsets.append(step)
+            pass_on(len(offsets) - 1, step)
+        if spread:
+            while relayed < len(offsets) - 2:
+                relay(relayed, offsets[relayed])
+                relayed += 1
+    if spread:
+        while relayed < len(offsets):
+            relay(relayed, offsets[relayed])
+            relayed += 1
+    for step in range(1, steps + 1):
+        for way in (1, -1):
+            hop(way, step).wait_send()
+    for order, offset in sent:
+        for step in range(sides):
+            send(order, offset, step).wait_send()
+        for step in range(1, sides):
+            forward(order, offset, step, core).wait_send()
+            forward(order, offset, step, 1 - core).wait_recv()
+        beside_in(order, offset).wait_recv()
+    own.wait()
+
+
+def ring_gather(value, axis, spread, collective_id):
+    size = lax.axis_size(axis)
+    sides = lax.axis_size("ulysses")
+    shape = (size,) + value.shape
+    if spread:
+        shape = (sides * 2,) + shape
+    space = pl.ANY if spread else pltpu.VMEM
+    hops = pltpu.SemaphoreType.DMA((2, size // 2 + 1))
+    across = pltpu.SemaphoreType.DMA((size, sides))
+    beside = pltpu.SemaphoreType.DMA((size,))
+    return pl.pallas_call(
+        functools.partial(ring_kernel, axis, spread),
+        out_shape=jax.ShapeDtypeStruct(shape, value.dtype),
+        in_specs=[pl.BlockSpec(memory_space=space)],
+        out_specs=pl.BlockSpec(memory_space=space),
+        scratch_shapes=[hops, hops, across, across, beside, beside, across, across]
+        + [pltpu.SemaphoreType.DMA],
+        compiler_params=pltpu.CompilerParams(collective_id=collective_id, has_side_effects=True),
+        cost_estimate=pl.CostEstimate(
+            flops=0, bytes_accessed=8 * math.prod(shape) + 4000000, transcendentals=0
+        ),
     )(value)
 
 
@@ -267,9 +444,11 @@
     if size % 2 == 0:
         half = rows // 2 if size > 2 else rows
         far = lax.rem(me + size // 2, size)
-        whole = place(whole, lax.ppermute(upward[:half], axis, up), far, 0)
+        upward = lax.ppermute(upward[:half], axis, up)
+        whole = place(whole, upward, far, 0)
         if half < rows:
-            whole = place(whole, lax.ppermute(downward[half:], axis, down), far, half)
+            downward = lax.ppermute(downward[half:], axis, down)
+            whole = place(whole, downward, far, half)
     return whole
 
 
@@ -310,13 +489,12 @@
         everyone,
         False,
         0,
-        "gather_time",
     )
     time_embed = first[:, :, :time_width].transpose(1, 0, 2).reshape(prompts, -1)
     lengths = first[:branches, :, time_width].astype(jnp.int32)
     acted = jax.nn.silu(time_embed[None] + pooled).astype(jnp.bfloat16)
     mod_part = jnp.einsum("bpd,dc->bpc", acted, mod_weight, preferred_element_type=jnp.float32)
-    mod_all = direct(mod_part, everyone, False, 1, "gather_mod")
+    mod_all = direct(mod_part, everyone, False, 1)
     own_mod = lax.dynamic_index_in_dim(mod_all, branch, 1, keepdims=False)
     own_mod = own_mod.transpose(1, 0, 2).reshape(prompts, 10, model_width)
     image_rows = img_tokens[0]
@@ -325,9 +503,8 @@
     slot_count = text_rows.shape[1]
     h_img = modulate(image_rows, own_mod[:, 0:1], own_mod[:, 1:2])
     h_txt = modulate(text_rows, own_mod[:, 4:5], own_mod[:, 3:4])
-    rows_all = quad_gather(
-        jnp.concatenate([h_img, h_txt], axis=1), 2, "gather_rows"
-    )
+    rows_own = jnp.concatenate([h_img, h_txt], axis=1)
+    rows_all = quad_gather(rows_own, 2)
     rows_all = rows_all.reshape(sides, branches, prompts, token_count + slot_count, model_width)
     rows_img = rows_all[:, :, :, :token_count]
     rows_txt = rows_all[:, :, :, token_count:]
@@ -343,7 +520,7 @@
     inner_local = queries.shape[-1]
     head_count = inner_local // head_size
     own_kv = jnp.concatenate([img_kv, txt_kv], axis=4)
-    all_kv = lax.all_gather(own_kv, "blk", axis=0, tiled=False)
+    all_kv = ring_gather(own_kv, "blk", False, 6)
     span = token_count + slot_count
     all_kv = all_kv.reshape(
         blocks, 2, sides, branches, prompts, span, head_count, head_size
@@ -381,22 +558,22 @@
     out_terms = out_terms.astype(jnp.bfloat16).reshape(
         sides * branches, prompts * token_count, model_width
     )
-    out_terms = direct(out_terms, near, True, 3, "swap_out")
+    out_terms = direct(out_terms, near, True, 3)
     attended = jnp.sum(out_terms.astype(jnp.float32), axis=0)
     attended = attended.reshape(prompts, token_count, model_width)
     residual = image_rows.astype(jnp.float32) + own_mod[:, 2:3] * attended
     feed_input = modulate(residual, own_mod[:, 7:8], own_mod[:, 8:9]).reshape(
         prompts * token_count, model_width
     )
-    feed_blocks = lax.all_gather(feed_input, "blk", axis=0, tiled=False)
-    feed_all = quad_gather(feed_blocks, 4, "gather_feed").reshape(-1, model_width)
+    feed_halves = feed_input.reshape(2, -1, model_width)
+    feed_all = ring_gather(feed_halves, "blk", True, 4).reshape(-1, model_width)
     pre_active = jnp.dot(feed_all, expand_full, preferred_element_type=jnp.float32)
     feed_hidden = jax.nn.gelu(pre_active, approximate=True).astype(jnp.bfloat16)
     feed_terms = jnp.dot(feed_hidden, reduce_weight, preferred_element_type=jnp.float32)
     feed_terms = feed_terms.astype(jnp.bfloat16).reshape(
         sides * branches * blocks, prompts * token_count, -1
     )
-    feed_terms = direct(feed_terms, ("ulysses", "cfg", "blk"), True, 5, "swap_feed")
+    feed_terms = direct(feed_terms, ("ulysses", "cfg", "blk"), True, 5)
     feed_terms = feed_terms.reshape(sides * branches, blocks, prompts * token_count, -1)
     feed_out = jnp.sum(feed_terms.astype(jnp.float32), axis=0).transpose(1, 0, 2)
     second_residual = residual + own_mod[:, 9:10] * feed_out.reshape(
@@ -433,4 +610,6 @@
         P(),
     )
     out_specs = P("groups", None, ("blk", "ulysses", "cfg"), None)
+
+
     return jax.shard_map(body, mesh=mesh, in_specs=in_specs, out_specs=out_specs, check_vma=False)

time: 437 us -> 430 us (0.984)
  Pallas kernels: 123 us -> 270 us
  waiting for transfers between devices: 154 us -> 10.8 us
  between operations: 15.4 us -> 1.81 us
    pallas_call x0 -> x2, Pallas kernels: none -> 104 us  [ring_gather(): pl.pallas_call(functools.partial(ring_kernel, axis, spread), out_shape=ja...]
    all_gather x2 -> x0, waiting for transfers between devices: 99 us -> none  [the longest x1 99 us: body(): all_kv = lax.all_gather(own_kv, 'blk', axis=0, tiled=False)]
    pallas_call x4, Pallas kernels: 70.6 us -> 153 us  [direct(): pl.pallas_call(functools.partial(direct_kernel, axes, swap), out_shape=ja...]
    ppermute x2, waiting for transfers between devices: 53.8 us -> 9.68 us  [the longest x1 9.68 us: ring_rows(): downward = lax.ppermute(downward[half:], axis, down)]
    pallas_call x2 -> x1, Pallas kernels: 52.3 us -> 13 us  [quad_gather(): pl.pallas_call(functools.partial(quad_kernel, chunks), out_shape=jax.Shap...]
    unnamed x36 -> x20, local copies, waits for them, and re-layouts: 10.1 us -> 9.53 us
  transfers between devices with their start and end apart: 7 -> 5, of which waited for: 4 -> 2; matrix products, arithmetic and copies ran while one was open for 15% -> 24% of each run, Pallas kernels for 4% -> 55%
where the time goes in v2:
time: 430 us; the launch traced here: 428 us
  Pallas kernels  270 us (63%)
  local copies, waits for them, and re-layouts  62.3 us (14%)
  matrix products  48.6 us (11%)
  other arithmetic  25.4 us (6%)
  waiting for transfers between devices  10.8 us (3%)
  starting transfers between devices  9.26 us (2%)
    pallas_call x4, Pallas kernels, direct(): pl.pallas_call(functools.partial(direct_kernel, axes, swap), out_shape=ja...  153 us
    pallas_call x2, Pallas kernels, ring_gather(): pl.pallas_call(functools.partial(ring_kernel, axis, spread), out_shape=ja...  104 us
    dot_general x1, matrix products, body(): jnp.dot(feed_hidden, reduce_weight, preferred_element_type=jnp.float32)  18.6 us
    pallas_call x1, Pallas kernels, quad_gather(): pl.pallas_call(functools.partial(quad_kernel, chunks), out_shape=jax.Shap...  13 us
    dynamic_update_slice x5, local copies, waits for them, and re-layouts, place(): lax.dynamic_update_slice_in_dim(whole, part, owner * rows + offset, 0)  11.1 us
    ppermute x1, waiting for transfers between devices, ring_rows(): downward = lax.ppermute(downward[half:], axis, down)  9.68 us
    unnamed x20, local copies, waits for them, and re-layouts  9.53 us
  transfers between devices with their start and end apart: 5, of which 2 were waited for; matrix products, arithmetic and copies ran while one was open for 24% of the time, Pallas kernels for 55%

profile of v2, /device:TPU:0, one launch (start us, length us, event | category | flops | bytes accessed | tf_op | source)
XLA Modules:
  0.0 428.5 jit_solution(6697016222691923879)
XLA Ops:
  0.0 3.1 collective-permute-start
  3.1 2.1 collective-permute-start.1
  5.9 1.6 convolution_reduce_fusion
  8.1 1.4 fusion.95
  9.5 0.7 pad_maximum_fusion.1.x_ref
  10.2 91.2 %shard_map.136 = f32[16,1,153]{2,1,0:T(1,128)} custom-call(f32[1,153]{1,0:T(1,128)} %pad_maximum_fusion.1.x_ref), custom_call_target="tpu_custom_call" | custom-call | bytes 4009792 | tf_op jit(solution)/shard_map/pallas_call | solution.py:126
  101.5 0.8 slice_reduce_fusion
  102.3 0.8 fusion.79
  103.1 5.1 %fusion.84 = f32[2,1520]{1,0:T(2,128)S(1)} fusion(bf16[2432,1520]{0,1:T(8,128)(2,1)} %param.21, bf16[2,1,2432]{2,1,0:T(2,128)(2,1)S(1)} %fusion.79), kind=kOutput, calls=%fused_computation.113 | convolution fusion | flops 14786560 | bytes 7415168 | tf_op jit(solution)/shard_map/bpd,dc->bpc/dot_general | solution.py:496
  108.9 8.4 %shard_map.137 = f32[16,2,1,1520]{3,2,1,0:T(1,128)} custom-call(f32[2,1,1520]{2,1,0:T(1,128)} %dot_general.55.x_ref), custom_call_target="tpu_custom_call" | custom-call | bytes 4194560 | tf_op jit(solution)/shard_map/pallas_call | solution.py:126
  117.3 1.2 dynamic-slice_reduce_fusion
  119.9 0.8 pad_maximum_fusion.x_ref
  120.7 13.0 %shard_map.138 = bf16[4,1,70,2432]{3,2,1,0:T(8,128)(2,1)} custom-call(bf16[1,70,2432]{2,1,0:T(8,128)(2,1)} %pad_maximum_fusion.x_ref), custom_call_target="tpu_custom_call" | custom-call | bytes 9447680 | tf_op jit(solution)/shard_map/pallas_call | solution.py:227
  133.7 5.7 %fusion.27 = f32[3,2,2,1,64,512]{5,4,3,2,1,0:T(8,128)S(1)} fusion(bf16[5,2432,512]{2,1,0:T(8,128)(2,1)} %param.22, bf16[2,2,1,70,2432]{4,3,1,0,2:T(8,128)(2,1)} %bitcast.210), kind=kOutput, calls=%fused_computation.30 | convolution fusion | flops 1912602624 | bytes 10289152 | tf_op jit(solution)/shard_map/ubprd,jdc->jubprc/dot_general | solution.py:511
  139.4 3.9 fusion.35
  143.4 0.7 slice.181
  144.2 0.9 convert_reduce_fusion.4
  145.1 1.2 mul.515
  146.3 1.6 reduce_sum.137
  148.1 1.3 mul.516
  149.4 2.3 mul.517
  152.3 2.4 slice_multiply_fusion.2
  154.7 0.9 fusion.78
  155.6 1.8 maximum_maximum_fusion.x_ref
  157.4 45.7 %shard_map.139 = bf16[4,2,2,2,1,70,512]{6,5,4,3,2,1,0:T(8,128)(2,1)} custom-call(bf16[2,2,2,1,70,512]{5,4,3,2,1,0:T(8,128)(2,1)} %maximum_maximum_fusion.x_ref), custom_call_target="tpu_custom_call" | custom-call | bytes 13175040 | tf_op jit(solution)/shard_map/pallas_call | solution.py:412
  203.0 6.8 %reshape.1179 = bf16[4,2,2,2,1,70,8,64]{7,6,5,3,2,1,0,4:T(8,128)(2,1)} reshape(bf16[4,2,2,2,1,70,512]{6,5,4,3,2,1,0:T(8,128)(2,1)} %shard_map.139) | data formatting | bytes 4587520 | tf_op jit(solution)/shard_map/reshape | solution.py:525
  209.9 4.8 %fusion.92 = (bf16[4,1,2,2,1,70,8,64]{7,6,5,3,2,1,0,4:T(8,128)(2,1)}, bf16[4,1,2,2,1,70,8,64]{7,6,5,3,2,1,0,4:T(8,128)(2,1)}) fusion(bf16[4,2,2,2,1,70,8,64]{7,6,5,3,2,1,0,4:T(8,128)(2,1)} %reshape.1179), kind=kLoop, calls=%fused_computation.151 | loop fusion | bytes 4587520 | tf_op jit(solution)/shard_map/slice | solution.py:534
  214.7 4.6 %copy.75 = bf16[4,1,2,2,1,70,8,64]{5,7,2,0,6,3,4,1:T(8,128)(2,1)} copy(bf16[4,1,2,2,1,70,8,64]{7,6,5,3,2,1,0,4:T(8,128)(2,1)} %get-tuple-element.17) | data formatting | bytes 2293760
  219.3 2.2 mul.508
  221.5 2.2 reduce_sum.136
  223.7 1.0 copy.49
  224.7 1.2 reshape_squeeze.2
  226.1 3.8 fusion.3
  229.9 4.0 fusion.12
  233.9 4.8 %copy.76 = bf16[4,1,2,2,1,70,8,64]{5,7,0,2,6,3,4,1:T(8,128)(2,1)} copy(bf16[4,1,2,2,1,70,8,64]{7,6,5,3,2,1,0,4:T(8,128)(2,1)} %get-tuple-element.18) | data formatting | bytes 2293760
  238.6 4.1 fusion.44
  243.1 1.0 reshape.1182
  244.1 2.8 convolution_convert_fusion
  247.0 17.5 %shard_map.140 = bf16[4,64,2432]{2,1,0:T(8,128)(2,1)} custom-call(bf16[4,64,2432]{2,1,0:T(8,128)(2,1)} %bitcast.208), custom_call_target="tpu_custom_call" | custom-call | bytes 6490368 | tf_op jit(solution)/shard_map/pallas_call | solution.py:126
  264.5 1.5 convert_reduce_fusion.1
  266.6 2.3 slice.131
  268.9 0.8 collective-permute-start.2
  269.8 0.9 add_convert_fusion.x_ref
  270.7 58.6 %shard_map.141 = bf16[4,4,2,32,2432]{4,3,2,1,0:T(8,128)(2,1)} custom-call(bf16[2,32,2432]{2,1,0:T(8,128)(2,1)} %add_convert_fusion.x_ref), custom_call_target="tpu_custom_call" | custom-call | bytes 23922944 | tf_op jit(solution)/shard_map/pallas_call | solution.py:412
  329.3 1.3 slice.132
  330.6 3.2 collective-permute-start.3
  333.9 3.9 broadcast_in_dim.23
  337.8 1.5 constant_dynamic-update-slice_fusion.4
  339.3 3.1 constant_dynamic-update-slice_fusion.3
  342.4 3.1 constant_dynamic-update-slice_fusion.2
  345.5 2.3 constant_dynamic-update-slice_fusion.1
  347.8 9.7 %collective-permute-done.3 = bf16[304,1792]{1,0:T(8,128)(2,1)S(1)} collective-permute-done((bf16[304,1792]{1,0:T(8,128)(2,1)S(1)}, bf16[304,1792]{1,0:T(8,128)(2,1)S(1)}, u32[]{:S(2)}, u32[]{:S(2)}) %collective-permute-start.3) | collective-permute-done | bytes 1089568 | tf_op jit(solution)/shard_map/ppermute | solution.py:450
  357.5 1.1 constant_dynamic-update-slice_fusion
  358.6 18.6 %fusion.24 = bf16[1024,608]{0,1:T(8,128)(2,1)S(1)} fusion(bf16[1792,608]{0,1:T(8,128)(2,1)} %param.25, bf16[1024,2432]{1,0:T(8,128)(2,1)} %bitcast.207, bf16[2432,1792]{1,0:T(8,128)(2,1)} %constant_dynamic-update-slice_fusion), kind=kOutput, calls=%fused_computation.29 | convolution fusion | flops 11173986304 | bytes 17121280 | tf_op jit(solution)/shard_map/dot_general | solution.py:572
  377.2 1.7 copy.60
  378.9 35.9 %shard_map.142 = bf16[16,64,608]{2,1,0:T(8,128)(2,1)} custom-call(bf16[16,64,608]{2,1,0:T(8,128)(2,1)} %bitcast.205), custom_call_target="tpu_custom_call" | custom-call | bytes 6490368 | tf_op jit(solution)/shard_map/pallas_call | solution.py:126
  414.8 1.6 convert_reduce_fusion
  416.4 1.3 copy.61
  417.7 2.3 reshape.1187
  420.0 2.3 reshape.1186
  422.2 1.3 fusion.69
  423.5 1.3 multiply_reduce_fusion
  424.9 1.5 convolution_bitcast_fusion
  426.7 1.1 collective-permute-done.4
  (77 shorter events, 5.2 us)
Async XLA Ops:
  0.0 244.1 %copy-start = (bf16[512,2432]{1,0:T(8,128)(2,1)S(1)}, bf16[512,2432]{1,0:T(8,128)(2,1)}, u32[]{:S(2)}) copy-start(bf16[512,2432]{1,0:T(8,128)(2,1)} %param.23) | copy-start | bytes 7471108
  0.0 266.6 %collective-permute-start = (bf16[608,1792]{1,0:T(8,128)(2,1)}, bf16[608,1792]{1,0:T(8,128)(2,1)}, u32[]{:S(2)}, u32[]{:S(2)}) collective-permute-start(bf16[608,1792]{1,0:T(8,128)(2,1)} %param.24), channel_id=1, source_target_pairs={{0,4},{4,8},{8,12},{12,0},{1,5},{5,9},{9,13},{13,1},{2,6},{6,10},{... | collective-permute-start | bytes 6537224 | tf_op jit(solution)/shard_map/ppermute | solution.py:440
  3.1 326.3 %collective-permute-start.1 = (bf16[608,1792]{1,0:T(8,128)(2,1)}, bf16[608,1792]{1,0:T(8,128)(2,1)}, u32[]{:S(2)}, u32[]{:S(2)}) collective-permute-start(bf16[608,1792]{1,0:T(8,128)(2,1)} %param.24), channel_id=1, source_target_pairs={{0,12},{4,0},{8,4},{12,8},{1,13},{5,1},{9,5},{13,9},{2,14},{6,2},{... | collective-permute-start | bytes 6537224 | tf_op jit(solution)/shard_map/ppermute | solution.py:441
  102.2 16.6 %copy-start.2 = (bf16[1,1,64,2432]{3,2,1,0:T(8,128)(2,1)S(1)}, bf16[1,1,64,2432]{3,2,1,0:T(8,128)(2,1)}, u32[]{:S(2)}) copy-start(bf16[1,1,64,2432]{3,2,1,0:T(8,128)(2,1)} %param.14) | copy-start | bytes 933892
  103.1 16.1 %copy-start.5 = (bf16[1,1,6,2432]{3,2,1,0:T(8,128)(2,1)S(1)}, bf16[1,1,6,2432]{3,2,1,0:T(8,128)(2,1)}, u32[]{:S(2)}) copy-start(bf16[1,1,6,2432]{3,2,1,0:T(8,128)(2,1)} %param.15) | copy-start | bytes 87556
  139.4 4.0 copy-start.4
  143.3 0.8 copy-start.6
  143.4 8.3 %copy-start.7 = (f32[3,64]{1,0:T(4,128)S(1)}, f32[3,64]{1,0:T(4,128)}, u32[]{:S(2)}) copy-start(f32[3,64]{1,0:T(4,128)} %param.26) | copy-start | bytes 2308
  268.9 76.6 %collective-permute-start.2 = (bf16[304,1792]{1,0:T(8,128)(2,1)}, bf16[304,1792]{1,0:T(8,128)(2,1)}, u32[]{:S(2)}, u32[]{:S(2)}) collective-permute-start(bf16[304,1792]{1,0:T(8,128)(2,1)} %slice.131), channel_id=1, source_target_pairs={{0,4},{4,8},{8,12},{12,0},{1,5},{5,9},{9,13},{13,1},{2,6},{6,10},{... | collective-permute-start | bytes 3268616 | tf_op jit(solution)/shard_map/ppermute | solution.py:447
  330.6 7.2 %copy-start.3 = (bf16[608,1792]{1,0:T(8,128)(2,1)S(1)}, bf16[608,1792]{1,0:T(8,128)(2,1)}, u32[]{:S(2)}) copy-start(bf16[608,1792]{1,0:T(8,128)(2,1)} %param.24) | copy-start | bytes 6537220
  330.6 26.8 %collective-permute-start.3 = (bf16[304,1792]{1,0:T(8,128)(2,1)S(1)}, bf16[304,1792]{1,0:T(8,128)(2,1)S(1)}, u32[]{:S(2)}, u32[]{:S(2)}) collective-permute-start(bf16[304,1792]{1,0:T(8,128)(2,1)S(1)} %slice.132), channel_id=1, source_target_pairs={{0,12},{4,0},{8,4},{12,8},{1,13},{5,1},{9,5},{13,9},{2,14},{6,2},{... | collective-permute-start | bytes 3268616 | tf_op jit(solution)/shard_map/ppermute | solution.py:450
  416.4 12.0 %copy-start.1 = (bf16[512,2432]{1,0:T(8,128)(2,1)S(1)}, bf16[512,2432]{1,0:T(8,128)(2,1)}, u32[]{:S(2)}) copy-start(bf16[512,2432]{1,0:T(8,128)(2,1)} %param.23) | copy-start | bytes 7471108
  426.6 1.2 collective-permute-start.4

commit v3 on v2

--- a/solution.py
+++ b/solution.py
@@ -42,9 +42,177 @@
 
 def rms_heads(values, gain):
     head_size = gain.shape[0]
-    shaped = values.reshape(values.shape[:-1] + (values.shape[-1] // head_size, head_size))
-    inverse = lax.rsqrt(jnp.mean(shaped * shaped, axis=-1, keepdims=True) + RMS_EPS)
-    return (shaped * inverse * gain).reshape(values.shape).astype(jnp.bfloat16)
+    width = values.shape[-1]
+    head_of = jnp.arange(width, dtype=jnp.int32) // head_size
+    same_head = (head_of[:, None] == head_of[None, :]).astype(jnp.float32) / head_size
+    mean_square = jnp.dot(
+        values * values,
+        same_head,
+        precision=lax.Precision.HIGHEST,
+        preferred_element_type=jnp.float32,
+    )
+    gains = jnp.tile(gain, width // head_size)
+    return (values * lax.rsqrt(mean_square + RMS_EPS) * gains).astype(jnp.bfloat16)
+
+
+def attention_kernel(head_size, q_ref, kv_ref, allowed_ref, o_ref):
+    sides, batch, rows, width = q_ref.shape
+    blocks, _, _, span, _ = kv_ref.shape
+    lanes = 2 * head_size
+    scale = 1.0 / math.sqrt(head_size)
+    low = lax.broadcasted_iota(jnp.int32, (1, lanes), 1) < head_size
+    for item in range(batch):
+        allowed = allowed_ref[item] > 0.0
+        for first in range(0, width, lanes):
+            here = slice(first, first + lanes)
+            queries = q_ref[:, item, :, here].reshape(sides * rows, lanes)
+            keys = kv_ref[:, 0, item, :, here].reshape(blocks * span, lanes)
+            values = kv_ref[:, 1, item, :, here].reshape(blocks * span, lanes)
+            mixed = []
+            for chosen in (low, jnp.logical_not(low)):
+                one_head = jnp.where(chosen, queries, jnp.zeros_like(queries))
+                scores = (
+                    lax.dot_general(
+                        one_head,
+                        keys,
+                        (((1,), (1,)), ((), ())),
+                        preferred_element_type=jnp.float32,
+                    )
+                    * scale
+                )
+                scores = jnp.where(allowed, scores, NEG_FILL)
+                largest = jnp.max(scores, axis=1, keepdims=True)
+                weights = jnp.where(allowed, jnp.exp(scores - largest), 0.0)
+                denominator = jnp.sum(weights, axis=1, keepdims=True)
+                update = jnp.dot(
+                    weights.astype(jnp.bfloat16), values, preferred_element_type=jnp.float32
+                )
+                mixed.append(update / denominator)
+            both = jnp.where(low, mixed[0], mixed[1]).astype(jnp.bfloat16)
+            o_ref[:, item, :, here] = both.reshape(sides, rows, lanes)
+
+
+def attention(queries, all_kv, allowed, head_size):
+    sides, batch, rows, width = queries.shape
+    keys = all_kv.shape[0] * all_kv.shape[3]
+    products = batch * sides * rows * keys * width
+    return pl.pallas_call(
+        functools.partial(attention_kernel, head_size),
+        out_shape=jax.ShapeDtypeStruct(queries.shape, jnp.bfloat16),
+        in_specs=[pl.BlockSpec(memory_space=pltpu.VMEM)] * 3,
+        out_specs=pl.BlockSpec(memory_space=pltpu.VMEM),
+        cost_estimate=pl.CostEstimate(
+            flops=8 * products,
+            bytes_accessed=4 * batch * keys * width + 4 * batch * sides * rows * width,
+            transcendentals=products // head_size,
+        ),
+        name="attention",
+    )(queries, all_kv, allowed)
+
+
+def reduce_kernel(axes, x_ref, o_ref, got, mine, core_s, core_r, far_s, far_r):
+    count = count_of(axes)
+    me = flat_position(axes)
+    core = lax.axis_index("cfg")
+    partner = {"cfg": 1 - core}
+    barrier = pltpu.get_barrier_semaphore()
+    pl.semaphore_signal(barrier, inc=1, device_id=partner, device_id_type=MESH)
+
+    def target(step):
+        return lax.rem(me + step, count)
+
+    def greet(step, carry):
+        pl.semaphore_signal(
+            barrier, inc=1, device_id=coordinates(target(step), axes), device_id_type=MESH
+        )
+        return carry
+
+    lax.fori_loop(1, count, greet, 0)
+    pl.semaphore_wait(barrier, count)
+
+    def beside(step):
+        slot = target(step)
+        return pltpu.make_async_remote_copy(
+            src_ref=x_ref.at[1 - core, slot],
+            dst_ref=got.at[slot],
+            send_sem=core_s.at[slot],
+            recv_sem=core_r.at[slot],
+            device_id=partner,
+            device_id_type=MESH,
+        )
+
+    def far(step):
+        slot = target(step)
+        return pltpu.make_async_remote_copy(
+            src_ref=mine.at[slot],
+            dst_ref=o_ref.at[me],
+            send_sem=far_s.at[step],
+            recv_sem=far_r.at[step],
+            device_id=coordinates(slot, axes),
+            device_id_type=MESH,
+        )
+
+    def far_in(step):
+        source = lax.rem(me - step + count, count)
+        return pltpu.make_async_remote_copy(
+            src_ref=mine.at[source],
+            dst_ref=o_ref.at[source],
+            send_sem=far_s.at[step],
+            recv_sem=far_r.at[step],
+            device_id=coordinates(source, axes),
+            device_id_type=MESH,
+        )
+
+    def total(slot):
+        beside_sum = x_ref[core, slot].astype(jnp.float32) + got[slot].astype(jnp.float32)
+        return beside_sum.astype(jnp.bfloat16)
+
+    def begin(step, carry):
+        beside(step).start()
+        return carry
+
+    def send(step, carry):
+        beside(step).wait_recv()
+        mine[target(step)] = total(target(step))
+        far(step).start()
+        return carry
+
+    def finish(step, carry):
+        far_in(step).wait_recv()
+        far(step).wait_send()
+        beside(step).wait_send()
+        return carry
+
+    lax.fori_loop(1, count + 1, begin, 0)
+    lax.fori_loop(1, count, send, 0)
+    beside(0).wait_recv()
+    o_ref[me] = total(me)
+    lax.fori_loop(1, count, finish, 0)
+    beside(0).wait_send()
+
+
+def reduce_cores(value, axes, collective_id):
+    shape = value.shape[1:]
+    count = shape[0]
+    sems = pltpu.SemaphoreType.DMA((count,))
+    return pl.pallas_call(
+        functools.partial(reduce_kernel, axes),
+        out_shape=jax.ShapeDtypeStruct(shape, value.dtype),
+        in_specs=[pl.BlockSpec(memory_space=pltpu.VMEM)],
+        out_specs=pl.BlockSpec(memory_space=pltpu.VMEM),
+        scratch_shapes=[
+            pltpu.VMEM(shape, value.dtype),
+            pltpu.VMEM(shape, value.dtype),
+            sems,
+            sems,
+            sems,
+            sems,
+        ],
+        compiler_params=pltpu.CompilerParams(collective_id=collective_id, has_side_effects=True),
+        cost_estimate=pl.CostEstimate(
+            flops=0, bytes_accessed=8 * math.prod(shape) + 4000000, transcendentals=0
+        ),
+    )(value)
 
 
 def flat_position(axes):
@@ -423,33 +591,50 @@
     )(value)
 
 
-def ring_rows(piece, axis):
-    size = lax.axis_size(axis)
-    me = lax.axis_index(axis)
-    rows = piece.shape[0]
-    up = [(source, (source + 1) % size) for source in range(size)]
-    down = [(source, (source - 1) % size) for source in range(size)]
-    whole = jnp.zeros((size * rows,) + piece.shape[1:], piece.dtype)
-
-    def place(whole, part, owner, offset):
-        return lax.dynamic_update_slice_in_dim(whole, part, owner * rows + offset, 0)
-
-    whole = place(whole, piece, me, 0)
-    upward = downward = piece
-    for step in range(1, (size - 1) // 2 + 1):
-        upward = lax.ppermute(upward, axis, up)
-        downward = lax.ppermute(downward, axis, down)
-        whole = place(whole, upward, lax.rem(me - step + size, size), 0)
-        whole = place(whole, downward, lax.rem(me + step, size), 0)
-    if size % 2 == 0:
-        half = rows // 2 if size > 2 else rows
-        far = lax.rem(me + size // 2, size)
-        upward = lax.ppermute(upward[:half], axis, up)
-        whole = place(whole, upward, far, 0)
-        if half < rows:
-            downward = lax.ppermute(downward[half:], axis, down)
-            whole = place(whole, downward, far, half)
-    return whole
+class WeightRing:
+    def __init__(self, piece, axis, across):
+        self.axis, self.across = axis, across
+        self.size = lax.axis_size(axis)
+        self.parts = lax.axis_size(across)
+        self.me = lax.axis_index(axis)
+        self.part = lax.axis_index(across)
+        self.rows = piece.shape[0]
+        self.share = self.rows // self.parts
+        self.up = [(source, (source + 1) % self.size) for source in range(self.size)]
+        self.down = [(source, (source - 1) % self.size) for source in range(self.size)]
+        whole = jnp.zeros((self.size * self.rows,) + piece.shape[1:], piece.dtype)
+        self.whole = lax.dynamic_update_slice_in_dim(whole, piece, self.me * self.rows, 0)
+        own = lax.dynamic_slice_in_dim(piece, self.part * self.share, self.share, 0)
+        self.upward = self.downward = own
+
+    def place(self, block, owner, offset):
+        for step in range(self.parts):
+            if step:
+                pairs = [(part, (part + step) % self.parts) for part in range(self.parts)]
+                moved = lax.ppermute(block, self.across, pairs)
+            else:
+                moved = block
+            origin = lax.rem(self.part - step + self.parts, self.parts)
+            start = owner * self.rows + origin * self.share + offset
+            self.whole = lax.dynamic_update_slice_in_dim(self.whole, moved, start, 0)
+
+    def hop(self, step, after):
+        size, me = self.size, self.me
+        self.upward, self.downward, after = lax.optimization_barrier(
+            (self.upward, self.downward, after)
+        )
+        if step <= (size - 1) // 2:
+            self.upward = lax.ppermute(self.upward, self.axis, self.up)
+            self.downward = lax.ppermute(self.downward, self.axis, self.down)
+            self.place(self.upward, lax.rem(me - step + size, size), 0)
+            self.place(self.downward, lax.rem(me + step, size), 0)
+        else:
+            half = self.share // 2
+            far = lax.rem(me + step, size)
+            low = lax.ppermute(self.upward[:half], self.axis, self.up)
+            high = lax.ppermute(self.downward[half:], self.axis, self.down)
+            self.place(jnp.concatenate([low, high], axis=0), far, 0)
+        return after
 
 
 def body(
@@ -470,14 +655,12 @@
 ):
     model_width = img_tokens.shape[3]
     prompts = img_tokens.shape[1]
-    head_size = qk_gain.shape[1]
     branches = pooled.shape[0]
     branch = lax.axis_index("cfg")
     everyone = ("blk", "ulysses", "cfg")
-    near = ("ulysses", "cfg")
     blocks = lax.axis_size("blk")
     sides = lax.axis_size("ulysses")
-    expand_full = ring_rows(expand_weight, "blk")
+    ring = WeightRing(expand_weight, "blk", "groups")
     sinusoid_rows = sinusoid(timestep, time_weight.shape[0]).astype(jnp.bfloat16)
     time_hidden = jax.nn.silu(
         jnp.dot(sinusoid_rows, time_weight, preferred_element_type=jnp.float32)
@@ -495,6 +678,7 @@
     acted = jax.nn.silu(time_embed[None] + pooled).astype(jnp.bfloat16)
     mod_part = jnp.einsum("bpd,dc->bpc", acted, mod_weight, preferred_element_type=jnp.float32)
     mod_all = direct(mod_part, everyone, False, 1)
+    mod_all = ring.hop(1, mod_all)
     own_mod = lax.dynamic_index_in_dim(mod_all, branch, 1, keepdims=False)
     own_mod = own_mod.transpose(1, 0, 2).reshape(prompts, 10, model_width)
     image_rows = img_tokens[0]
@@ -514,51 +698,38 @@
     txt_proj = jnp.einsum(
         "ubprd,jdc->jubprc", rows_txt, proj_weight[3:5], preferred_element_type=jnp.float32
     )
-    queries = rms_heads(img_proj[0], qk_gain[0])
-    img_kv = jnp.stack([rms_heads(img_proj[1], qk_gain[1]), img_proj[2].astype(jnp.bfloat16)])
-    txt_kv = jnp.stack([rms_heads(txt_proj[0], qk_gain[2]), txt_proj[1].astype(jnp.bfloat16)])
-    inner_local = queries.shape[-1]
-    head_count = inner_local // head_size
-    own_kv = jnp.concatenate([img_kv, txt_kv], axis=4)
+    batch = branches * prompts
+    inner_local = img_proj.shape[-1]
+    queries = rms_heads(img_proj[0], qk_gain[0]).reshape(sides, batch, token_count, inner_local)
+
+    def by_item(keys, values):
+        pair = jnp.stack([keys, values]).reshape(2, sides, batch, -1, inner_local)
+        return pair.transpose(0, 2, 1, 3, 4).reshape(2, batch, -1, inner_local)
+
+    img_kv = by_item(rms_heads(img_proj[1], qk_gain[1]), img_proj[2].astype(jnp.bfloat16))
+    txt_kv = by_item(rms_heads(txt_proj[0], qk_gain[2]), txt_proj[1].astype(jnp.bfloat16))
+    img_span = img_kv.shape[2]
+    txt_span = txt_kv.shape[2]
+    padding = -txt_span % 16
+    own_kv = jnp.concatenate(
+        [img_kv, jnp.pad(txt_kv, ((0, 0), (0, 0), (0, padding), (0, 0)))], axis=2
+    )
     all_kv = ring_gather(own_kv, "blk", False, 6)
-    span = token_count + slot_count
-    all_kv = all_kv.reshape(
-        blocks, 2, sides, branches, prompts, span, head_count, head_size
-    )
-    query_heads = queries.reshape(sides, branches, prompts, token_count, head_count, head_size)
-    scale = 1.0 / math.sqrt(head_size)
-    scores = (
-        jnp.einsum(
-            "ubpqhd,zvbpkhd->bphuqzvk",
-            query_heads,
-            all_kv[:, 0],
-            preferred_element_type=jnp.float32,
-        )
-        * scale
-    )
-    place = jnp.arange(span, dtype=jnp.int32) - token_count
-    slot = (
-        jnp.arange(blocks * sides, dtype=jnp.int32).reshape(blocks, sides, 1) * slot_count + place
-    )
-    allowed = (place < 0) | (slot < lengths[:, :, None, None, None])
-    allowed = allowed[:, :, None, None, None]
-    scores = jnp.where(allowed, scores, NEG_FILL)
-    largest = jnp.max(scores, axis=(5, 6, 7), keepdims=True)
-    weights = jnp.where(allowed, jnp.exp(scores - largest), 0.0)
-    denominator = jnp.sum(weights, axis=(5, 6, 7))
-    mixed = jnp.einsum(
-        "bphuqzvk,zvbpkhd->bphuqd",
-        weights.astype(jnp.bfloat16),
-        all_kv[:, 1],
-        preferred_element_type=jnp.float32,
-    )
-    mixed = (mixed / denominator[..., None]).astype(jnp.bfloat16)
-    mixed_rows = mixed.transpose(3, 0, 1, 4, 2, 5).reshape(-1, inner_local)
-    out_terms = jnp.dot(mixed_rows, out_weight, preferred_element_type=jnp.float32)
+    for step in range(2, blocks // 2 + 1):
+        all_kv = ring.hop(step, all_kv)
+    place = jnp.arange(img_span + txt_span + padding, dtype=jnp.int32) - img_span
+    slot = jnp.arange(blocks, dtype=jnp.int32)[:, None] * txt_span + place
+    live = (slot < lengths.reshape(batch, 1, 1)) & (place < txt_span)
+    allowed = ((place < 0) | live).astype(jnp.float32).reshape(batch, 1, -1)
+    mixed = attention(queries, all_kv, allowed, qk_gain.shape[1])
+    out_terms = jnp.dot(
+        mixed.reshape(-1, inner_local), out_weight, preferred_element_type=jnp.float32
+    )
     out_terms = out_terms.astype(jnp.bfloat16).reshape(
-        sides * branches, prompts * token_count, model_width
-    )
-    out_terms = direct(out_terms, near, True, 3)
+        sides, branches, prompts * token_count, model_width
+    )
+    out_terms = out_terms.transpose(1, 0, 2, 3)
+    out_terms = reduce_cores(out_terms, ("ulysses",), 3)
     attended = jnp.sum(out_terms.astype(jnp.float32), axis=0)
     attended = attended.reshape(prompts, token_count, model_width)
     residual = image_rows.astype(jnp.float32) + own_mod[:, 2:3] * attended
@@ -566,15 +737,19 @@
         prompts * token_count, model_width
     )
     feed_halves = feed_input.reshape(2, -1, model_width)
-    feed_all = ring_gather(feed_halves, "blk", True, 4).reshape(-1, model_width)
-    pre_active = jnp.dot(feed_all, expand_full, preferred_element_type=jnp.float32)
+    feed_all = ring_gather(feed_halves, "blk", True, 4)
+    feed_all = feed_all.reshape(-1, model_width)
+    pre_active = jnp.dot(feed_all, ring.whole, preferred_element_type=jnp.float32)
     feed_hidden = jax.nn.gelu(pre_active, approximate=True).astype(jnp.bfloat16)
     feed_terms = jnp.dot(feed_hidden, reduce_weight, preferred_element_type=jnp.float32)
     feed_terms = feed_terms.astype(jnp.bfloat16).reshape(
-        sides * branches * blocks, prompts * token_count, -1
-    )
-    feed_terms = direct(feed_terms, ("ulysses", "cfg", "blk"), True, 5)
-    feed_terms = feed_terms.reshape(sides * branches, blocks, prompts * token_count, -1)
+        sides, branches, blocks, prompts * token_count, -1
+    )
+    feed_terms = feed_terms.transpose(1, 0, 2, 3, 4).reshape(
+        branches, sides * blocks, prompts * token_count, -1
+    )
+    feed_terms = reduce_cores(feed_terms, ("ulysses", "blk"), 5)
+    feed_terms = feed_terms.reshape(sides, blocks, prompts * token_count, -1)
     feed_out = jnp.sum(feed_terms.astype(jnp.float32), axis=0).transpose(1, 0, 2)
     second_residual = residual + own_mod[:, 9:10] * feed_out.reshape(
         prompts, token_count, model_width

time: 430 us -> 298 us (0.69)
  Pallas kernels: 270 us -> 163 us
  local copies, waits for them, and re-layouts: 62.3 us -> 37.1 us
  other arithmetic: 25.4 us -> 13.4 us
  waiting for transfers between devices: 10.8 us -> 21.2 us
    pallas_call x4 -> x2, Pallas kernels: 153 us -> 19.5 us  [direct(): pl.pallas_call(functools.partial(direct_kernel, axes, swap), out_shape=ja...]
    pallas_call x0 -> x3, Pallas kernels: none -> 41.3 us  [the longest x2 33.9 us: reduce_cores(): pl.pallas_call(functools.partial(reduce_kernel, axes), out_shape=jax.Shap...]
    pallas_call x2, Pallas kernels: 104 us -> 88.8 us  [ring_gather(): pl.pallas_call(functools.partial(ring_kernel, axis, spread), out_shape=ja...]
    ppermute x4 -> x7, waiting for transfers between devices: 9.69 us -> 20.4 us  [the longest x1 9.21 us: hop(): high = lax.ppermute(self.downward[half:], self.axis, self.down)]
    unnamed x20 -> x19, local copies, waits for them, and re-layouts: 9.53 us -> 1.21 us
    reduce_sum x4 -> x0, other arithmetic: 7.9 us -> none  [the longest x1 4 us: body(): denominator = jnp.sum(weights, axis=(5, 6, 7))]
    mul x13 -> x3, local copies, waits for them, and re-layouts: 7.5 us -> 0.23 us  [rms_heads(): values * lax.rsqrt(mean_square + RMS_EPS) * gains]
    reshape x2, local copies, waits for them, and re-layouts: 7.86 us -> 1.21 us  [the longest x1 1.2 us: body(): out_terms.astype(jnp.bfloat16)]
  transfers between devices with their start and end apart: 5 -> 8, of which waited for: 2 -> 4; matrix products, arithmetic and copies ran while one was open for 24% -> 16% of each run, Pallas kernels for 55% -> 34%
where the time goes in v3:
time: 298 us; the launch traced here: 297 us
  Pallas kernels  163 us (55%)
  matrix products  48.1 us (16%)
  local copies, waits for them, and re-layouts  37.1 us (12%)
  waiting for transfers between devices  21.2 us (7%)
  other arithmetic  13.4 us (4%)
  starting transfers between devices  12.5 us (4%)
    pallas_call x2, Pallas kernels, ring_gather(): pl.pallas_call(functools.partial(ring_kernel, axis, spread), out_shape=ja...  88.8 us
    pallas_call x2, Pallas kernels, reduce_cores(): pl.pallas_call(functools.partial(reduce_kernel, axes), out_shape=jax.Shap...  33.9 us
    dot_general x1, matrix products, body(): jnp.dot(feed_hidden, reduce_weight, preferred_element_type=jnp.float32)  19.6 us
    pallas_call x2, Pallas kernels, direct(): pl.pallas_call(functools.partial(direct_kernel, axes, swap), out_shape=ja...  19.5 us
    pallas_call x1, Pallas kernels, quad_gather(): pl.pallas_call(functools.partial(quad_kernel, chunks), out_shape=jax.Shap...  13.1 us
    dynamic_update_slice x6, local copies, waits for them, and re-layouts, place(): self.whole = lax.dynamic_update_slice_in_dim(self.whole, moved, start, 0)  11.5 us
    ppermute x1, waiting for transfers between devices, hop(): high = lax.ppermute(self.downward[half:], self.axis, self.down)  9.21 us
    ppermute x1, waiting for transfers between devices, hop(): low = lax.ppermute(self.upward[:half], self.axis, self.up)  8.37 us
  transfers between devices with their start and end apart: 8, of which 4 were waited for; matrix products, arithmetic and copies ran while one was open for 16% of the time, Pallas kernels for 34%

profile of v3, /device:TPU:0, one launch (start us, length us, event | category | flops | bytes accessed | tf_op | source)
XLA Modules:
  0.0 296.8 jit_solution(3118699563872469923)
XLA Ops:
  0.9 1.6 convolution_reduce_fusion
  3.2 1.4 fusion.115
  4.6 0.7 pad_maximum_fusion.1.x_ref
  5.2 9.8 %shard_map.136 = f32[16,1,153]{2,1,0:T(1,128)} custom-call(f32[1,153]{1,0:T(1,128)} %pad_maximum_fusion.1.x_ref), custom_call_target="tpu_custom_call" | custom-call | bytes 4009792 | tf_op jit(solution)/shard_map/pallas_call | solution.py:294
  15.1 0.8 slice_reduce_fusion
  15.9 0.8 fusion.89
  16.7 5.1 %fusion.94 = f32[2,1520]{1,0:T(2,128)S(1)} fusion(bf16[2432,1520]{0,1:T(8,128)(2,1)} %param.21, bf16[2,1,2432]{2,1,0:T(2,128)(2,1)S(1)} %fusion.89), kind=kOutput, calls=%fused_computation.134 | convolution fusion | flops 14786560 | bytes 7415168 | tf_op jit(solution)/shard_map/bpd,dc->bpc/dot_general | solution.py:679
  21.8 0.6 dot_general.58.x_ref
  22.5 9.6 %shard_map.137 = f32[16,2,1,1520]{3,2,1,0:T(1,128)} custom-call(f32[2,1,1520]{2,1,0:T(1,128)} %dot_general.58.x_ref), custom_call_target="tpu_custom_call" | custom-call | bytes 4194560 | tf_op jit(solution)/shard_map/pallas_call | solution.py:294
  32.1 2.3 constant_dynamic-slice_fusion.2
  34.4 1.9 collective-permute-start
  36.3 2.0 collective-permute-start.1
  38.2 1.1 dynamic-slice_reduce_fusion
  40.9 0.8 pad_maximum_fusion.x_ref
  41.7 13.1 %shard_map.138 = bf16[4,1,70,2432]{3,2,1,0:T(8,128)(2,1)} custom-call(bf16[1,70,2432]{2,1,0:T(8,128)(2,1)} %pad_maximum_fusion.x_ref), custom_call_target="tpu_custom_call" | custom-call | bytes 9447680 | tf_op jit(solution)/shard_map/pallas_call | solution.py:395
  54.8 6.9 %fusion.19 = f32[3,2,2,1,64,512]{5,4,2,1,3,0:T(8,128)} fusion(bf16[5,2432,512]{2,1,0:T(8,128)(2,1)} %param.22, bf16[2,2,1,70,2432]{4,3,1,0,2:T(8,128)(2,1)} %bitcast.212), kind=kOutput, calls=%fused_computation.18 | convolution fusion | flops 1912602624 | bytes 10289152 | tf_op jit(solution)/shard_map/ubprd,jdc->jubprc/dot_general | solution.py:695
  61.7 4.0 %fusion.32 = f32[2,2,2,1,6,512]{5,4,0,2,1,3:T(8,128)} fusion(bf16[5,2432,512]{2,1,0:T(8,128)(2,1)} %param.22, bf16[2,2,1,70,2432]{4,3,1,0,2:T(8,128)(2,1)} %bitcast.213), kind=kOutput, calls=%fused_computation.36 | convolution fusion | flops 119537664 | bytes 5234688 | tf_op jit(solution)/shard_map/ubprd,jdc->jubprc/dot_general | solution.py:698
  65.8 1.1 slice.185
  66.9 2.4 fusion.31
  69.6 0.8 slice.186
  70.4 1.7 fusion.39
  72.2 0.9 fusion.57.x_ref
  73.1 53.0 %shard_map.139.kv_ref = bf16[4,2,2,144,512]{4,3,2,1,0:T(8,128)(2,1)} custom-call(bf16[2,2,144,512]{3,2,1,0:T(8,128)(2,1)} %fusion.57.x_ref), custom_call_target="tpu_custom_call" | custom-call | bytes 13437184 | tf_op jit(solution)/shard_map/pallas_call | solution.py:580
  126.7 0.8 convert_reduce_fusion.4
  127.5 0.7 or_convert_fusion.allowed_ref
  128.2 3.1 %fusion.28.q_ref = bf16[2,2,64,512]{3,2,1,0:T(8,128)(2,1)} fusion(s32[512]{0:T(512)S(1)} %add_select_fusion, f32[3,2,2,1,64,512]{5,4,2,1,3,0:T(8,128)} %fusion.19, f32[512]{0:T(512)S(1)} %mul.428), kind=kOutput, calls=%fused_computation.31 | convolution fusion | flops 806486016 | bytes 1316864 | tf_op jit(solution)/shard_map/dot_general | solution.py:48
  131.3 3.9 %broadcast_in_dim.2 = bf16[2432,1792]{1,0:T(8,128)(2,1)} broadcast(bf16[]{:T(256)} %constant.110.clone.1), dimensions={} | broadcast | bytes 8716290 | tf_op jit(solution)/shard_map/broadcast_in_dim | solution.py:605
  135.2 1.5 constant_dynamic-update-slice_fusion.8
  136.7 7.4 %attention.1 = bf16[2,2,64,512]{3,2,1,0:T(8,128)(2,1)} custom-call(bf16[2,2,64,512]{3,2,1,0:T(8,128)(2,1)} %fusion.28.q_ref, bf16[4,2,2,144,512]{4,3,2,1,0:T(8,128)(2,1)} %shard_map.139.kv_ref, f32[2,1,576]{2,1,0:T(1,128)} %or_convert_fusion.allowed_ref), custom_call_target="tpu_custom_call" | custom-call | flops 603979776 | bytes 2883584 | tf_op jit(solution)/shard_map/attention/pallas_call | solution.py:99
  144.1 1.8 convolution_convert_fusion
  145.9 1.2 copy.67
  147.1 13.4 %shard_map.140 = bf16[2,64,2432]{2,1,0:T(8,128)(2,1)} custom-call(bf16[2,2,64,2432]{3,2,1,0:T(8,128)(2,1)} %bitcast.208), custom_call_target="tpu_custom_call" | custom-call | bytes 6490368 | tf_op jit(solution)/shard_map/pallas_call | solution.py:198
  160.6 1.2 convert_reduce_fusion.1
  162.3 1.1 slice.102
  163.4 0.5 collective-permute-start.4
  163.9 1.9 slice.103
  165.8 3.4 %collective-permute-start.5 = (bf16[152,1792]{1,0:T(8,128)(2,1)}, bf16[152,1792]{1,0:T(8,128)(2,1)}, u32[]{:S(2)}, u32[]{:S(2)}) collective-permute-start(bf16[152,1792]{1,0:T(8,128)(2,1)} %slice.103), channel_id=1, source_target_pairs={{0,12},{4,0},{8,4},{12,8},{1,13},{5,1},{9,5},{13,9},{2,14},{6,2},{... | collective-permute-start | bytes 1634312 | tf_op jit(solution)/shard_map/ppermute | solution.py:635
  169.3 1.5 collective-permute-start.2
  170.8 0.9 add_convert_fusion.x_ref
  172.3 8.4 %collective-permute-done.4 = bf16[152,1792]{1,0:T(8,128)(2,1)} collective-permute-done((bf16[152,1792]{1,0:T(8,128)(2,1)S(1)}, bf16[152,1792]{1,0:T(8,128)(2,1)}, u32[]{:S(2)}, u32[]{:S(2)}) %collective-permute-start.4) | collective-permute-done | bytes 544800 | tf_op jit(solution)/shard_map/ppermute | solution.py:634
  180.6 1.1 constant_dynamic-update-slice_fusion.1
  181.7 9.2 %collective-permute-done.5 = bf16[152,1792]{1,0:T(8,128)(2,1)} collective-permute-done((bf16[152,1792]{1,0:T(8,128)(2,1)}, bf16[152,1792]{1,0:T(8,128)(2,1)}, u32[]{:S(2)}, u32[]{:S(2)}) %collective-permute-start.5) | collective-permute-done | bytes 544800 | tf_op jit(solution)/shard_map/ppermute | solution.py:635
  190.9 1.1 constant_dynamic-update-slice_fusion
  192.0 1.6 collective-permute-start.6
  193.6 2.3 constant_dynamic-update-slice_fusion.7
  195.9 35.8 %shard_map.141 = bf16[4,4,2,32,2432]{4,3,2,1,0:T(8,128)(2,1)} custom-call(bf16[2,32,2432]{2,1,0:T(8,128)(2,1)} %add_convert_fusion.x_ref), custom_call_target="tpu_custom_call" | custom-call | bytes 23922944 | tf_op jit(solution)/shard_map/pallas_call | solution.py:580
  231.7 2.4 constant_dynamic-update-slice_fusion.6
  234.1 2.3 constant_dynamic-update-slice_fusion.5
  236.4 1.1 constant_dynamic-update-slice_fusion.4
  237.5 1.0 constant_dynamic-update-slice_fusion.3
  238.6 2.8 collective-permute-done.6
  241.3 2.3 constant_dynamic-update-slice_fusion.2
  243.7 19.6 %fusion.16 = bf16[1024,608]{0,1:T(8,128)(2,1)} fusion(bf16[1792,608]{0,1:T(8,128)(2,1)} %param.25, bf16[1024,2432]{1,0:T(8,128)(2,1)} %bitcast.206, bf16[2432,1792]{1,0:T(8,128)(2,1)} %constant_dynamic-update-slice_fusion.2), kind=kOutput, calls=%fused_computation.17 | convolution fusion | flops 11173986304 | bytes 17121280 | tf_op jit(solution)/shard_map/dot_general | solution.py:744
  263.3 1.7 copy.45
  265.0 1.2 copy.46
  266.2 20.5 %shard_map.142 = bf16[8,64,608]{2,1,0:T(8,128)(2,1)} custom-call(bf16[2,8,64,608]{3,2,1,0:T(8,128)(2,1)} %bitcast.205), custom_call_target="tpu_custom_call" | custom-call | bytes 6490368 | tf_op jit(solution)/shard_map/pallas_call | solution.py:198
  286.7 1.3 convert_reduce_fusion
  288.4 1.2 reshape.1194
  289.5 1.2 reshape.1193
  290.7 1.5 fusion.80
  292.2 1.3 multiply_reduce_fusion
  294.1 1.2 collective-permute-start.7
  295.4 0.8 collective-permute-done.7
  296.2 0.6 multiply_add_fusion.1
  (79 shorter events, 4.7 us)
Async XLA Ops:
  0.0 144.1 %copy-start = (bf16[512,2432]{1,0:T(8,128)(2,1)S(1)}, bf16[512,2432]{1,0:T(8,128)(2,1)}, u32[]{:S(2)}) copy-start(bf16[512,2432]{1,0:T(8,128)(2,1)} %param.23) | copy-start | bytes 7471108
  21.8 18.0 %copy-start.2 = (bf16[1,1,64,2432]{3,2,1,0:T(8,128)(2,1)S(1)}, bf16[1,1,64,2432]{3,2,1,0:T(8,128)(2,1)}, u32[]{:S(2)}) copy-start(bf16[1,1,64,2432]{3,2,1,0:T(8,128)(2,1)} %param.14) | copy-start | bytes 933892
  21.8 18.4 %copy-start.5 = (bf16[1,1,6,2432]{3,2,1,0:T(8,128)(2,1)S(1)}, bf16[1,1,6,2432]{3,2,1,0:T(8,128)(2,1)}, u32[]{:S(2)}) copy-start(bf16[1,1,6,2432]{3,2,1,0:T(8,128)(2,1)} %param.15) | copy-start | bytes 87556
  34.4 102.3 %collective-permute-start = (bf16[304,1792]{1,0:T(8,128)(2,1)}, bf16[304,1792]{1,0:T(8,128)(2,1)}, u32[]{:S(2)}, u32[]{:S(2)}) collective-permute-start(bf16[304,1792]{1,0:T(8,128)(2,1)} %constant_dynamic-slice_fusion.2), channel_id=1, source_target_pairs={{0,4},{4,8},{8,12},{12,0},{1,5},{5,9},{9,13},{13,1},{2,6},{6,10},{... | collective-permute-start | bytes 3268616 | tf_op jit(solution)/shard_map/ppermute | solution.py:627
  36.3 100.4 %collective-permute-start.1 = (bf16[304,1792]{1,0:T(8,128)(2,1)}, bf16[304,1792]{1,0:T(8,128)(2,1)}, u32[]{:S(2)}, u32[]{:S(2)}) collective-permute-start(bf16[304,1792]{1,0:T(8,128)(2,1)} %constant_dynamic-slice_fusion.2), channel_id=1, source_target_pairs={{0,12},{4,0},{8,4},{12,8},{1,13},{5,1},{9,5},{13,9},{2,14},{6,2},{... | collective-permute-start | bytes 3268616 | tf_op jit(solution)/shard_map/ppermute | solution.py:628
  61.7 4.1 %copy-start.7 = (f32[3,64]{1,0:T(4,128)S(1)}, f32[3,64]{1,0:T(4,128)}, u32[]{:S(2)}) copy-start(f32[3,64]{1,0:T(4,128)} %param.26) | copy-start | bytes 2308
  131.3 3.9 %copy-start.3 = (bf16[608,1792]{1,0:T(8,128)(2,1)S(1)}, bf16[608,1792]{1,0:T(8,128)(2,1)}, u32[]{:S(2)}) copy-start(bf16[608,1792]{1,0:T(8,128)(2,1)} %param.24) | copy-start | bytes 6537220
  163.4 17.2 %collective-permute-start.4 = (bf16[152,1792]{1,0:T(8,128)(2,1)S(1)}, bf16[152,1792]{1,0:T(8,128)(2,1)}, u32[]{:S(2)}, u32[]{:S(2)}) collective-permute-start(bf16[152,1792]{1,0:T(8,128)(2,1)S(1)} %slice.102), channel_id=1, source_target_pairs={{0,4},{4,8},{8,12},{12,0},{1,5},{5,9},{9,13},{13,1},{2,6},{6,10},{... | collective-permute-start | bytes 1634312 | tf_op jit(solution)/shard_map/ppermute | solution.py:634
  165.8 25.1 %collective-permute-start.5 = (bf16[152,1792]{1,0:T(8,128)(2,1)}, bf16[152,1792]{1,0:T(8,128)(2,1)}, u32[]{:S(2)}, u32[]{:S(2)}) collective-permute-start(bf16[152,1792]{1,0:T(8,128)(2,1)} %slice.103), channel_id=1, source_target_pairs={{0,12},{4,0},{8,4},{12,8},{1,13},{5,1},{9,5},{13,9},{2,14},{6,2},{... | collective-permute-start | bytes 1634312 | tf_op jit(solution)/shard_map/ppermute | solution.py:635
  169.3 62.4 %collective-permute-start.2 = (bf16[304,1792]{1,0:T(8,128)(2,1)}, bf16[304,1792]{1,0:T(8,128)(2,1)}, u32[]{:S(2)}, u32[]{:S(2)}) collective-permute-start(bf16[304,1792]{1,0:T(8,128)(2,1)} %collective-permute-done), channel_id=1, source_target_pairs={{0,16},{16,0},{1,17},{17,1},{2,18},{18,2},{3,19},{19,3},{4,20},{20... | collective-permute-start | bytes 3268616 | tf_op jit(solution)/shard_map/ppermute | solution.py:614
  171.8 64.7 %collective-permute-start.3 = (bf16[304,1792]{1,0:T(8,128)(2,1)}, bf16[304,1792]{1,0:T(8,128)(2,1)S(1)}, u32[]{:S(2)}, u32[]{:S(2)}) collective-permute-start(bf16[304,1792]{1,0:T(8,128)(2,1)} %collective-permute-done.1), channel_id=1, source_target_pairs={{0,16},{16,0},{1,17},{17,1},{2,18},{18,2},{3,19},{19,3},{4,20},{20... | collective-permute-start | bytes 3268616 | tf_op jit(solution)/shard_map/ppermute | solution.py:614
  192.0 49.3 %collective-permute-start.6 = (bf16[304,1792]{1,0:T(8,128)(2,1)S(1)}, bf16[304,1792]{1,0:T(8,128)(2,1)}, u32[]{:S(2)}, u32[]{:S(2)}) collective-permute-start(bf16[304,1792]{1,0:T(8,128)(2,1)S(1)} %constant_dynamic-update-slice_fusion), channel_id=1, source_target_pairs={{0,16},{16,0},{1,17},{17,1},{2,18},{18,2},{3,19},{19,3},{4,20},{20... | collective-permute-start | bytes 3268616 | tf_op jit(solution)/shard_map/ppermute | solution.py:614
  290.7 2.8 copy-start.4
  290.7 2.8 copy-start.6
  290.7 6.1 %copy-start.1 = (bf16[512,2432]{1,0:T(8,128)(2,1)S(1)}, bf16[512,2432]{1,0:T(8,128)(2,1)}, u32[]{:S(2)}) copy-start(bf16[512,2432]{1,0:T(8,128)(2,1)} %param.23) | copy-start | bytes 7471108
  294.1 2.0 collective-permute-start.7

commit v4 on v3

--- a/solution.py
+++ b/solution.py
@@ -115,6 +115,7 @@
     me = flat_position(axes)
     core = lax.axis_index("cfg")
     partner = {"cfg": 1 - core}
+    inner = x_ref.shape[2]
     barrier = pltpu.get_barrier_semaphore()
     pl.semaphore_signal(barrier, inc=1, device_id=partner, device_id_type=MESH)
 
@@ -133,7 +134,7 @@
     def beside(step):
         slot = target(step)
         return pltpu.make_async_remote_copy(
-            src_ref=x_ref.at[1 - core, slot],
+            src_ref=x_ref.at[slot // inner, 1 - core, lax.rem(slot, inner)],
             dst_ref=got.at[slot],
             send_sem=core_s.at[slot],
             recv_sem=core_r.at[slot],
@@ -164,7 +165,8 @@
         )
 
     def total(slot):
-        beside_sum = x_ref[core, slot].astype(jnp.float32) + got[slot].astype(jnp.float32)
+        own = x_ref[slot // inner, core, lax.rem(slot, inner)]
+        beside_sum = own.astype(jnp.float32) + got[slot].astype(jnp.float32)
         return beside_sum.astype(jnp.bfloat16)
 
     def begin(step, carry):
@@ -192,8 +194,8 @@
 
 
 def reduce_cores(value, axes, collective_id):
-    shape = value.shape[1:]
-    count = shape[0]
+    count = value.shape[0] * value.shape[2]
+    shape = (count,) + value.shape[3:]
     sems = pltpu.SemaphoreType.DMA((count,))
     return pl.pallas_call(
         functools.partial(reduce_kernel, axes),
@@ -726,9 +728,8 @@
         mixed.reshape(-1, inner_local), out_weight, preferred_element_type=jnp.float32
     )
     out_terms = out_terms.astype(jnp.bfloat16).reshape(
-        sides, branches, prompts * token_count, model_width
-    )
-    out_terms = out_terms.transpose(1, 0, 2, 3)
+        sides, branches, 1, prompts * token_count, model_width
+    )
     out_terms = reduce_cores(out_terms, ("ulysses",), 3)
     attended = jnp.sum(out_terms.astype(jnp.float32), axis=0)
     attended = attended.reshape(prompts, token_count, model_width)
@@ -741,12 +742,10 @@
     feed_all = feed_all.reshape(-1, model_width)
     pre_active = jnp.dot(feed_all, ring.whole, preferred_element_type=jnp.float32)
     feed_hidden = jax.nn.gelu(pre_active, approximate=True).astype(jnp.bfloat16)
+    feed_hidden = lax.optimization_barrier(feed_hidden)
     feed_terms = jnp.dot(feed_hidden, reduce_weight, preferred_element_type=jnp.float32)
     feed_terms = feed_terms.astype(jnp.bfloat16).reshape(
         sides, branches, blocks, prompts * token_count, -1
-    )
-    feed_terms = feed_terms.transpose(1, 0, 2, 3, 4).reshape(
-        branches, sides * blocks, prompts * token_count, -1
     )
     feed_terms = reduce_cores(feed_terms, ("ulysses", "blk"), 5)
     feed_terms = feed_terms.reshape(sides, blocks, prompts * token_count, -1)

time: 298 us -> 294 us (0.987)
    dot_general x1, matrix products: 19.6 us -> 2.44 us  [body(): jnp.dot(feed_hidden, reduce_weight, preferred_element_type=jnp.float32)]
    dot_general x0 -> x1, matrix products: none -> 14.6 us  [body(): jnp.dot(feed_all, ring.whole, preferred_element_type=jnp.float32)]
  transfers between devices with their start and end apart: 8 -> 8, of which waited for: 4 -> 4; matrix products, arithmetic and copies ran while one was open for 16% -> 16% of each run, Pallas kernels for 34% -> 35%
where the time goes in v4:
time: 294 us; the launch traced here: 293 us
  Pallas kernels  163 us (55%)
  matrix products  46.6 us (16%)
  local copies, waits for them, and re-layouts  34.5 us (12%)
  waiting for transfers between devices  21.2 us (7%)
  other arithmetic  13.4 us (5%)
  starting transfers between devices  12.5 us (4%)
    pallas_call x2, Pallas kernels, ring_gather(): pl.pallas_call(functools.partial(ring_kernel, axis, spread), out_shape=ja...  88.8 us
    pallas_call x2, Pallas kernels, reduce_cores(): pl.pallas_call(functools.partial(reduce_kernel, axes), out_shape=jax.Shap...  33.9 us
    pallas_call x2, Pallas kernels, direct(): pl.pallas_call(functools.partial(direct_kernel, axes, swap), out_shape=ja...  19.5 us
    dot_general x1, matrix products, body(): jnp.dot(feed_all, ring.whole, preferred_element_type=jnp.float32)  14.6 us
    pallas_call x1, Pallas kernels, quad_gather(): pl.pallas_call(functools.partial(quad_kernel, chunks), out_shape=jax.Shap...  13.1 us
    dynamic_update_slice x6, local copies, waits for them, and re-layouts, place(): self.whole = lax.dynamic_update_slice_in_dim(self.whole, moved, start, 0)  11.5 us
    ppermute x1, waiting for transfers between devices, hop(): high = lax.ppermute(self.downward[half:], self.axis, self.down)  9.21 us
    ppermute x1, waiting for transfers between devices, hop(): low = lax.ppermute(self.upward[:half], self.axis, self.up)  8.37 us
  transfers between devices with their start and end apart: 8, of which 4 were waited for; matrix products, arithmetic and copies ran while one was open for 16% of the time, Pallas kernels for 35%

profile of v4, /device:TPU:0, one launch (start us, length us, event | category | flops | bytes accessed | tf_op | source)
XLA Modules:
  0.0 292.7 jit_solution(17854230883293940945)
XLA Ops:
  0.9 1.6 convolution_reduce_fusion
  3.2 1.4 fusion.104
  4.6 0.7 pad_maximum_fusion.1.x_ref
  5.2 9.8 %shard_map.136 = f32[16,1,153]{2,1,0:T(1,128)} custom-call(f32[1,153]{1,0:T(1,128)} %pad_maximum_fusion.1.x_ref), custom_call_target="tpu_custom_call" | custom-call | bytes 4009792 | tf_op jit(solution)/shard_map/pallas_call | solution.py:296
  15.1 0.8 slice_reduce_fusion
  15.9 0.8 fusion.84
  16.7 5.1 %fusion.89 = f32[2,1520]{1,0:T(2,128)S(1)} fusion(bf16[2432,1520]{0,1:T(8,128)(2,1)} %param.21, bf16[2,1,2432]{2,1,0:T(2,128)(2,1)S(1)} %fusion.84), kind=kOutput, calls=%fused_computation.132 | convolution fusion | flops 14786560 | bytes 7415168 | tf_op jit(solution)/shard_map/bpd,dc->bpc/dot_general | solution.py:681
  21.8 0.6 dot_general.58.x_ref
  22.5 9.6 %shard_map.137 = f32[16,2,1,1520]{3,2,1,0:T(1,128)} custom-call(f32[2,1,1520]{2,1,0:T(1,128)} %dot_general.58.x_ref), custom_call_target="tpu_custom_call" | custom-call | bytes 4194560 | tf_op jit(solution)/shard_map/pallas_call | solution.py:296
  32.1 2.3 constant_dynamic-slice_fusion.2
  34.4 1.9 collective-permute-start
  36.3 2.0 collective-permute-start.1
  38.2 1.1 dynamic-slice_reduce_fusion
  40.9 0.8 pad_maximum_fusion.x_ref
  41.7 13.1 %shard_map.138 = bf16[4,1,70,2432]{3,2,1,0:T(8,128)(2,1)} custom-call(bf16[1,70,2432]{2,1,0:T(8,128)(2,1)} %pad_maximum_fusion.x_ref), custom_call_target="tpu_custom_call" | custom-call | bytes 9447680 | tf_op jit(solution)/shard_map/pallas_call | solution.py:397
  54.8 6.9 %fusion.14 = f32[3,2,2,1,64,512]{5,4,2,1,3,0:T(8,128)} fusion(bf16[5,2432,512]{2,1,0:T(8,128)(2,1)} %param.22, bf16[2,2,1,70,2432]{4,3,1,0,2:T(8,128)(2,1)} %bitcast.205), kind=kOutput, calls=%fused_computation.17 | convolution fusion | flops 1912602624 | bytes 10289152 | tf_op jit(solution)/shard_map/ubprd,jdc->jubprc/dot_general | solution.py:697
  61.7 4.0 %fusion.27 = f32[2,2,2,1,6,512]{5,4,0,2,1,3:T(8,128)} fusion(bf16[5,2432,512]{2,1,0:T(8,128)(2,1)} %param.22, bf16[2,2,1,70,2432]{4,3,1,0,2:T(8,128)(2,1)} %bitcast.206), kind=kOutput, calls=%fused_computation.34 | convolution fusion | flops 119537664 | bytes 5234688 | tf_op jit(solution)/shard_map/ubprd,jdc->jubprc/dot_general | solution.py:700
  65.8 1.1 slice.185
  66.9 2.4 fusion.26
  69.6 0.8 slice.186
  70.4 1.7 fusion.34
  72.2 0.9 fusion.52.x_ref
  73.1 53.0 %shard_map.139.kv_ref = bf16[4,2,2,144,512]{4,3,2,1,0:T(8,128)(2,1)} custom-call(bf16[2,2,144,512]{3,2,1,0:T(8,128)(2,1)} %fusion.52.x_ref), custom_call_target="tpu_custom_call" | custom-call | bytes 13437184 | tf_op jit(solution)/shard_map/pallas_call | solution.py:582
  126.7 0.8 convert_reduce_fusion.4
  127.5 0.7 or_convert_fusion.allowed_ref
  128.2 3.1 %fusion.23.q_ref = bf16[2,2,64,512]{3,2,1,0:T(8,128)(2,1)} fusion(s32[512]{0:T(512)S(1)} %add_select_fusion, f32[3,2,2,1,64,512]{5,4,2,1,3,0:T(8,128)} %fusion.14, f32[512]{0:T(512)S(1)} %mul.428), kind=kOutput, calls=%fused_computation.29 | convolution fusion | flops 806486016 | bytes 1316864 | tf_op jit(solution)/shard_map/dot_general | solution.py:48
  131.3 3.9 %broadcast_in_dim.2 = bf16[2432,1792]{1,0:T(8,128)(2,1)} broadcast(bf16[]{:T(256)} %constant.110.clone.1), dimensions={} | broadcast | bytes 8716290 | tf_op jit(solution)/shard_map/broadcast_in_dim | solution.py:607
  135.2 1.5 constant_dynamic-update-slice_fusion.8
  136.7 7.4 %attention.1 = bf16[2,2,64,512]{3,2,1,0:T(8,128)(2,1)} custom-call(bf16[2,2,64,512]{3,2,1,0:T(8,128)(2,1)} %fusion.23.q_ref, bf16[4,2,2,144,512]{4,3,2,1,0:T(8,128)(2,1)} %shard_map.139.kv_ref, f32[2,1,576]{2,1,0:T(1,128)} %or_convert_fusion.allowed_ref), custom_call_target="tpu_custom_call" | custom-call | flops 603979776 | bytes 2883584 | tf_op jit(solution)/shard_map/attention/pallas_call | solution.py:99
  144.1 2.9 convolution_convert_fusion
  147.1 13.4 %shard_map.140 = bf16[2,64,2432]{2,1,0:T(8,128)(2,1)} custom-call(bf16[2,2,1,64,2432]{4,3,2,1,0:T(8,128)(2,1)} %bitcast.201), custom_call_target="tpu_custom_call" | custom-call | bytes 6490368 | tf_op jit(solution)/shard_map/pallas_call | solution.py:200
  160.5 1.2 convert_reduce_fusion.1
  162.2 1.1 slice.102
  163.3 0.5 collective-permute-start.4
  163.8 1.9 slice.103
  165.8 3.4 %collective-permute-start.5 = (bf16[152,1792]{1,0:T(8,128)(2,1)}, bf16[152,1792]{1,0:T(8,128)(2,1)}, u32[]{:S(2)}, u32[]{:S(2)}) collective-permute-start(bf16[152,1792]{1,0:T(8,128)(2,1)} %slice.103), channel_id=1, source_target_pairs={{0,12},{4,0},{8,4},{12,8},{1,13},{5,1},{9,5},{13,9},{2,14},{6,2},{... | collective-permute-start | bytes 1634312 | tf_op jit(solution)/shard_map/ppermute | solution.py:637
  169.2 1.5 collective-permute-start.2
  170.8 0.9 add_convert_fusion.x_ref
  171.7 0.5 collective-permute-start.3
  172.2 8.4 %collective-permute-done.4 = bf16[152,1792]{1,0:T(8,128)(2,1)} collective-permute-done((bf16[152,1792]{1,0:T(8,128)(2,1)S(1)}, bf16[152,1792]{1,0:T(8,128)(2,1)}, u32[]{:S(2)}, u32[]{:S(2)}) %collective-permute-start.4) | collective-permute-done | bytes 544800 | tf_op jit(solution)/shard_map/ppermute | solution.py:636
  180.5 1.1 constant_dynamic-update-slice_fusion.1
  181.6 9.2 %collective-permute-done.5 = bf16[152,1792]{1,0:T(8,128)(2,1)} collective-permute-done((bf16[152,1792]{1,0:T(8,128)(2,1)}, bf16[152,1792]{1,0:T(8,128)(2,1)}, u32[]{:S(2)}, u32[]{:S(2)}) %collective-permute-start.5) | collective-permute-done | bytes 544800 | tf_op jit(solution)/shard_map/ppermute | solution.py:637
  190.8 1.1 constant_dynamic-update-slice_fusion
  191.9 1.6 collective-permute-start.6
  193.5 2.3 constant_dynamic-update-slice_fusion.7
  195.8 35.8 %shard_map.141 = bf16[4,4,2,32,2432]{4,3,2,1,0:T(8,128)(2,1)} custom-call(bf16[2,32,2432]{2,1,0:T(8,128)(2,1)} %add_convert_fusion.x_ref), custom_call_target="tpu_custom_call" | custom-call | bytes 23922944 | tf_op jit(solution)/shard_map/pallas_call | solution.py:582
  231.7 2.4 constant_dynamic-update-slice_fusion.6
  234.0 2.3 constant_dynamic-update-slice_fusion.5
  236.3 1.1 constant_dynamic-update-slice_fusion.4
  237.4 1.0 constant_dynamic-update-slice_fusion.3
  238.5 2.8 collective-permute-done.6
  241.3 2.3 constant_dynamic-update-slice_fusion.2
  243.6 14.6 %fusion.10 = bf16[1024,1792]{1,0:T(8,128)(2,1)S(1)} fusion(bf16[1024,2432]{1,0:T(8,128)(2,1)S(1)} %bitcast.200, bf16[2432,1792]{1,0:T(8,128)(2,1)} %constant_dynamic-update-slice_fusion.2), kind=kOutput, calls=%fused_computation.11 | convolution fusion | flops 8941993984 | bytes 17367040 | tf_op jit(solution)/shard_map/dot_general | solution.py:743
  258.2 2.4 convolution_convert_fusion.1
  260.6 1.5 copy.40
  262.1 20.5 %shard_map.142 = bf16[8,64,608]{2,1,0:T(8,128)(2,1)} custom-call(bf16[2,2,4,64,608]{4,3,2,1,0:T(8,128)(2,1)} %bitcast.199), custom_call_target="tpu_custom_call" | custom-call | bytes 6490368 | tf_op jit(solution)/shard_map/pallas_call | solution.py:200
  282.6 1.3 convert_reduce_fusion
  284.3 1.2 reshape.1190
  285.4 1.2 reshape.1189
  286.6 1.5 fusion.75
  288.1 1.3 multiply_reduce_fusion
  290.0 1.2 collective-permute-start.7
  291.3 0.8 collective-permute-done.7
  292.1 0.6 multiply_add_fusion.1
  (82 shorter events, 4.2 us)
Async XLA Ops:
  0.0 144.1 %copy-start = (bf16[512,2432]{1,0:T(8,128)(2,1)S(1)}, bf16[512,2432]{1,0:T(8,128)(2,1)}, u32[]{:S(2)}) copy-start(bf16[512,2432]{1,0:T(8,128)(2,1)} %param.23) | copy-start | bytes 7471108
  21.8 18.0 %copy-start.2 = (bf16[1,1,64,2432]{3,2,1,0:T(8,128)(2,1)S(1)}, bf16[1,1,64,2432]{3,2,1,0:T(8,128)(2,1)}, u32[]{:S(2)}) copy-start(bf16[1,1,64,2432]{3,2,1,0:T(8,128)(2,1)} %param.14) | copy-start | bytes 933892
  21.8 18.4 %copy-start.6 = (bf16[1,1,6,2432]{3,2,1,0:T(8,128)(2,1)S(1)}, bf16[1,1,6,2432]{3,2,1,0:T(8,128)(2,1)}, u32[]{:S(2)}) copy-start(bf16[1,1,6,2432]{3,2,1,0:T(8,128)(2,1)} %param.15) | copy-start | bytes 87556
  34.4 102.3 %collective-permute-start = (bf16[304,1792]{1,0:T(8,128)(2,1)}, bf16[304,1792]{1,0:T(8,128)(2,1)}, u32[]{:S(2)}, u32[]{:S(2)}) collective-permute-start(bf16[304,1792]{1,0:T(8,128)(2,1)} %constant_dynamic-slice_fusion.2), channel_id=1, source_target_pairs={{0,4},{4,8},{8,12},{12,0},{1,5},{5,9},{9,13},{13,1},{2,6},{6,10},{... | collective-permute-start | bytes 3268616 | tf_op jit(solution)/shard_map/ppermute | solution.py:629
  36.3 100.4 %collective-permute-start.1 = (bf16[304,1792]{1,0:T(8,128)(2,1)}, bf16[304,1792]{1,0:T(8,128)(2,1)}, u32[]{:S(2)}, u32[]{:S(2)}) collective-permute-start(bf16[304,1792]{1,0:T(8,128)(2,1)} %constant_dynamic-slice_fusion.2), channel_id=1, source_target_pairs={{0,12},{4,0},{8,4},{12,8},{1,13},{5,1},{9,5},{13,9},{2,14},{6,2},{... | collective-permute-start | bytes 3268616 | tf_op jit(solution)/shard_map/ppermute | solution.py:630
  61.7 4.1 %copy-start.8 = (f32[3,64]{1,0:T(4,128)S(1)}, f32[3,64]{1,0:T(4,128)}, u32[]{:S(2)}) copy-start(f32[3,64]{1,0:T(4,128)} %param.26) | copy-start | bytes 2308
  131.3 3.9 %copy-start.4 = (bf16[608,1792]{1,0:T(8,128)(2,1)S(1)}, bf16[608,1792]{1,0:T(8,128)(2,1)}, u32[]{:S(2)}) copy-start(bf16[608,1792]{1,0:T(8,128)(2,1)} %param.24) | copy-start | bytes 6537220
  163.3 17.2 %collective-permute-start.4 = (bf16[152,1792]{1,0:T(8,128)(2,1)S(1)}, bf16[152,1792]{1,0:T(8,128)(2,1)}, u32[]{:S(2)}, u32[]{:S(2)}) collective-permute-start(bf16[152,1792]{1,0:T(8,128)(2,1)S(1)} %slice.102), channel_id=1, source_target_pairs={{0,4},{4,8},{8,12},{12,0},{1,5},{5,9},{9,13},{13,1},{2,6},{6,10},{... | collective-permute-start | bytes 1634312 | tf_op jit(solution)/shard_map/ppermute | solution.py:636
  165.8 25.1 %collective-permute-start.5 = (bf16[152,1792]{1,0:T(8,128)(2,1)}, bf16[152,1792]{1,0:T(8,128)(2,1)}, u32[]{:S(2)}, u32[]{:S(2)}) collective-permute-start(bf16[152,1792]{1,0:T(8,128)(2,1)} %slice.103), channel_id=1, source_target_pairs={{0,12},{4,0},{8,4},{12,8},{1,13},{5,1},{9,5},{13,9},{2,14},{6,2},{... | collective-permute-start | bytes 1634312 | tf_op jit(solution)/shard_map/ppermute | solution.py:637
  169.2 62.4 %collective-permute-start.2 = (bf16[304,1792]{1,0:T(8,128)(2,1)}, bf16[304,1792]{1,0:T(8,128)(2,1)}, u32[]{:S(2)}, u32[]{:S(2)}) collective-permute-start(bf16[304,1792]{1,0:T(8,128)(2,1)} %collective-permute-done), channel_id=1, source_target_pairs={{0,16},{16,0},{1,17},{17,1},{2,18},{18,2},{3,19},{19,3},{4,20},{20... | collective-permute-start | bytes 3268616 | tf_op jit(solution)/shard_map/ppermute | solution.py:616
  171.7 64.7 %collective-permute-start.3 = (bf16[304,1792]{1,0:T(8,128)(2,1)}, bf16[304,1792]{1,0:T(8,128)(2,1)S(1)}, u32[]{:S(2)}, u32[]{:S(2)}) collective-permute-start(bf16[304,1792]{1,0:T(8,128)(2,1)} %collective-permute-done.1), channel_id=1, source_target_pairs={{0,16},{16,0},{1,17},{17,1},{2,18},{18,2},{3,19},{19,3},{4,20},{20... | collective-permute-start | bytes 3268616 | tf_op jit(solution)/shard_map/ppermute | solution.py:616
  191.9 49.3 %collective-permute-start.6 = (bf16[304,1792]{1,0:T(8,128)(2,1)S(1)}, bf16[304,1792]{1,0:T(8,128)(2,1)}, u32[]{:S(2)}, u32[]{:S(2)}) collective-permute-start(bf16[304,1792]{1,0:T(8,128)(2,1)S(1)} %constant_dynamic-update-slice_fusion), channel_id=1, source_target_pairs={{0,16},{16,0},{1,17},{17,1},{2,18},{18,2},{3,19},{19,3},{4,20},{20... | collective-permute-start | bytes 3268616 | tf_op jit(solution)/shard_map/ppermute | solution.py:616
  236.3 7.2 %copy-start.3 = (bf16[4,4,2,32,2432]{4,3,2,1,0:T(8,128)(2,1)S(1)}, bf16[4,4,2,32,2432]{4,3,2,1,0:T(8,128)(2,1)}, u32[]{:S(2)}) copy-start(bf16[4,4,2,32,2432]{4,3,2,1,0:T(8,128)(2,1)} %shard_map.141) | copy-start | bytes 14942212
  243.6 14.6 %copy-start.9 = (bf16[1792,608]{0,1:T(8,128)(2,1)S(1)}, bf16[1792,608]{0,1:T(8,128)(2,1)}, u32[]{:S(2)}) copy-start(bf16[1792,608]{0,1:T(8,128)(2,1)} %param.25) | copy-start | bytes 6537220
  286.6 2.8 copy-start.5
  286.6 2.8 copy-start.7
  286.6 6.1 %copy-start.1 = (bf16[512,2432]{1,0:T(8,128)(2,1)S(1)}, bf16[512,2432]{1,0:T(8,128)(2,1)}, u32[]{:S(2)}) copy-start(bf16[512,2432]{1,0:T(8,128)(2,1)} %param.23) | copy-start | bytes 7471108
  290.0 2.0 collective-permute-start.7
